TPU v7x, 32 devices: a 4x2x2 block of a 4x4x8 slice. The times are simulated.
32 devices in a mesh: dp: 4 (over y, z), sp: 8 (over x, core).
Axes of the slice: x: 4, y: 2, z: 2, core: 2. Of those that a mesh axis runs over, the one named last changes fastest.
The devices are a block of a 4x4x8 slice.
Arguments:
- x_in: bfloat16 [4, 3072, 2048], P('dp', 'sp'), parts along dimension 0
- d_out: bfloat16 [4, 3072, 2048], P('dp', 'sp'), parts along dimension 0
- gain: float32 [2048], replicated
- w_q: bfloat16 [2048, 32, 64], replicated
- w_k: bfloat16 [2048, 8, 64], replicated
- w_v: bfloat16 [2048, 8, 64], replicated
- w_o: bfloat16 [32, 64, 2048], replicated
Outputs:
- output 1: bfloat16 [4, 3072, 2048], P('dp', 'sp'), parts along dimension 0
- output 2: bfloat16 [4, 3072, 2048], P('dp', 'sp'), parts along dimension 0
- output 3: float32 [8192, 32, 64], P('dp'), parts along dimension 0
- output 4: float32 [8192, 8, 64], P('dp'), parts along dimension 0
- output 5: float32 [8192, 8, 64], P('dp'), parts along dimension 0
- output 6: float32 [128, 64, 2048], P('dp'), parts along dimension 0
- output 7: float32 [8192], P('dp'), parts along dimension 0
There are 4 independent parts. A program takes and returns all parts, laid end to end along the dimension named above; an argument that names none is the same for every part.
All inputs are finite; a program needn't handle non-finite values.
Results may differ from a plain program's by a relative error of at most 0.0122979.
Values are sent between devices in bfloat16 or wider.
A program may use at most 768 MiB of HBM per device.

v0:
```python
import math
import jax
import jax.numpy as jnp
from jax import lax
from jax.sharding import PartitionSpec as P

ROPE_BASE = 1000000.0
NORM_EPS = 1e-5


def rope_tables(positions, head_dim):
    half = head_dim // 2
    inv_freq = ROPE_BASE ** (-2.0 * jnp.arange(half, dtype=jnp.float32) / head_dim)
    angle = positions[:, None] * inv_freq[None, :]
    return jnp.cos(angle), jnp.sin(angle)


def rotate(t_val, cos_t, sin_t):
    half = t_val.shape[-1] // 2
    first = t_val[..., :half]
    second = t_val[..., half:]
    cos_b = cos_t[:, None, :]
    sin_b = sin_t[:, None, :]
    return jnp.concatenate([first * cos_b - second * sin_b, second * cos_b + first * sin_b], axis=-1)


def rotate_back(grad_val, cos_t, sin_t):
    half = grad_val.shape[-1] // 2
    first = grad_val[..., :half]
    second = grad_val[..., half:]
    cos_b = cos_t[:, None, :]
    sin_b = sin_t[:, None, :]
    return jnp.concatenate([first * cos_b + second * sin_b, second * cos_b - first * sin_b], axis=-1)


def norm_forward(x_local, gain):
    x_f32 = x_local.astype(jnp.float32)
    inv_rms = lax.rsqrt(jnp.mean(x_f32 * x_f32, axis=-1, keepdims=True) + NORM_EPS)
    x_hat = x_f32 * inv_rms
    return x_hat, inv_rms, (x_hat * gain).astype(jnp.bfloat16)


def norm_backward(d_normed, x_hat, inv_rms, gain):
    d_hat = d_normed * gain
    return inv_rms * (d_hat - x_hat * jnp.mean(d_hat * x_hat, axis=-1, keepdims=True))


def project(normed, w_q, w_k, w_v, cos_t, sin_t):
    q_lin = jnp.einsum('bsd,dhe->bshe', normed, w_q, preferred_element_type=jnp.float32)
    k_lin = jnp.einsum('bsd,dhe->bshe', normed, w_k, preferred_element_type=jnp.float32)
    v_lin = jnp.einsum('bsd,dhe->bshe', normed, w_v, preferred_element_type=jnp.float32)
    return rotate(q_lin, cos_t, sin_t).astype(jnp.bfloat16), rotate(k_lin, cos_t, sin_t).astype(jnp.bfloat16), v_lin.astype(jnp.bfloat16)


def project_back(dq_lin, dk_lin, dv_val, w_q, w_k, w_v):
    d_q = jnp.einsum('bshe,dhe->bsd', dq_lin, w_q, preferred_element_type=jnp.float32)
    d_k = jnp.einsum('bshe,dhe->bsd', dk_lin, w_k, preferred_element_type=jnp.float32)
    d_v = jnp.einsum('bshe,dhe->bsd', dv_val, w_v, preferred_element_type=jnp.float32)
    return (d_q + d_k + d_v).astype(jnp.bfloat16)


def block_length(seq_q, num_q):
    return math.gcd(seq_q, max(64, 8192 // num_q))


def attention_forward(q_heads, k_heads, v_heads, q_offset):
    batch, seq_q, num_q, head_dim = q_heads.shape
    seq_k, num_kv = k_heads.shape[1], k_heads.shape[2]
    group = num_q // num_kv
    block_len = block_length(seq_q, num_q)
    scale = head_dim ** -0.5
    q_grouped = q_heads.reshape(batch, seq_q, num_kv, group, head_dim)
    key_pos = jnp.arange(seq_k)

    def one_block(block_idx):
        start = block_idx * block_len
        q_rows = lax.dynamic_slice_in_dim(q_grouped, start, block_len, axis=1)
        scores = jnp.einsum('bqkgd,btkd->bkgqt', q_rows, k_heads, preferred_element_type=jnp.float32) * scale
        q_pos = q_offset + start + jnp.arange(block_len)
        scores = jnp.where(key_pos[None, :] <= q_pos[:, None], scores, -1e30)
        row_max = jnp.max(scores, axis=-1, keepdims=True)
        exp_scores = jnp.exp(scores - row_max)
        row_sum = jnp.sum(exp_scores, axis=-1, keepdims=True)
        attn_weights = (exp_scores / row_sum).astype(jnp.bfloat16)
        out_rows = jnp.einsum('bkgqt,btkd->bqkgd', attn_weights, v_heads, preferred_element_type=jnp.float32)
        return out_rows.astype(jnp.bfloat16), row_max + jnp.log(row_sum)

    out_blocks, log_sum = lax.map(one_block, jnp.arange(seq_q // block_len))
    return jnp.moveaxis(out_blocks, 0, 1).reshape(batch, seq_q, num_q, head_dim), log_sum


def attention_backward(q_heads, k_heads, v_heads, d_heads, log_sum, q_offset):
    batch, seq_q, num_q, head_dim = q_heads.shape
    seq_k, num_kv = k_heads.shape[1], k_heads.shape[2]
    group = num_q // num_kv
    block_len = block_length(seq_q, num_q)
    num_blocks = seq_q // block_len
    scale = head_dim ** -0.5
    q_grouped = q_heads.reshape(batch, seq_q, num_kv, group, head_dim)
    d_grouped = d_heads.reshape(batch, seq_q, num_kv, group, head_dim)
    key_pos = jnp.arange(seq_k)

    def one_block(carry, inputs):
        dk_acc, dv_acc = carry
        block_idx, lse_rows = inputs
        start = block_idx * block_len
        q_rows = lax.dynamic_slice_in_dim(q_grouped, start, block_len, axis=1)
        d_rows = lax.dynamic_slice_in_dim(d_grouped, start, block_len, axis=1)
        scores = jnp.einsum('bqkgd,btkd->bkgqt', q_rows, k_heads, preferred_element_type=jnp.float32) * scale
        q_pos = q_offset + start + jnp.arange(block_len)
        scores = jnp.where(key_pos[None, :] <= q_pos[:, None], scores, -1e30)
        attn_weights = jnp.exp(scores - lse_rows)
        d_weights = jnp.einsum('bqkgd,btkd->bkgqt', d_rows, v_heads, preferred_element_type=jnp.float32).astype(jnp.bfloat16)
        delta = jnp.sum(attn_weights * d_weights, axis=-1, keepdims=True)
        d_scores = (attn_weights * (d_weights - delta) * scale).astype(jnp.bfloat16)
        dq_rows = jnp.einsum('bkgqt,btkd->bqkgd', d_scores, k_heads, preferred_element_type=jnp.float32).astype(jnp.bfloat16)
        dk_acc = dk_acc + jnp.einsum('bkgqt,bqkgd->btkd', d_scores, q_rows, preferred_element_type=jnp.float32)
        dv_acc = dv_acc + jnp.einsum('bkgqt,bqkgd->btkd', attn_weights.astype(jnp.bfloat16), d_rows, preferred_element_type=jnp.float32)
        return (dk_acc, dv_acc), dq_rows

    zeros = jnp.zeros(k_heads.shape, jnp.float32)
    (dk_acc, dv_acc), dq_blocks = lax.scan(one_block, (zeros, zeros), (jnp.arange(num_blocks), log_sum))
    return jnp.moveaxis(dq_blocks, 0, 1).reshape(batch, seq_q, num_q, head_dim), dk_acc, dv_acc


def solution(mesh):
    seq_par = mesh.shape['sp']

    def local_step(x_local, dy_local, gain, w_q, w_k, w_v, w_o):
        batch, seq_loc, d_model = x_local.shape
        num_kv, head_dim = w_k.shape[1], w_k.shape[2]
        spread = max(num_kv, seq_par) // num_kv
        offset = lax.axis_index('sp') * seq_loc
        cos_t, sin_t = rope_tables((offset + jnp.arange(seq_loc)).astype(jnp.float32), head_dim)
        x_hat, inv_rms, normed = norm_forward(x_local, gain)
        q_rot, k_rot, v_val = project(normed, w_q, w_k, w_v, cos_t, sin_t)
        k_send = k_rot
        v_send = v_val
        if spread > 1:
            k_send = jnp.repeat(k_rot, spread, axis=2)
            v_send = jnp.repeat(v_val, spread, axis=2)
        q_heads = lax.all_to_all(q_rot, 'sp', 2, 1, tiled=True)
        k_heads = lax.all_to_all(k_send, 'sp', 2, 1, tiled=True)
        v_heads = lax.all_to_all(v_send, 'sp', 2, 1, tiled=True)
        o_heads, log_sum = attention_forward(q_heads, k_heads, v_heads, 0)
        o_local = lax.all_to_all(o_heads, 'sp', 1, 2, tiled=True)
        y_proj = jnp.einsum('bshe,hed->bsd', o_local, w_o, preferred_element_type=jnp.float32)
        y_out = (x_local.astype(jnp.float32) + y_proj).astype(jnp.bfloat16)
        d_o = jnp.einsum('bsd,hed->bshe', dy_local, w_o, preferred_element_type=jnp.float32).astype(jnp.bfloat16)
        d_wo = jnp.einsum('bshe,bsd->hed', o_local, dy_local, preferred_element_type=jnp.float32)
        d_o_heads = lax.all_to_all(d_o, 'sp', 2, 1, tiled=True)
        dq_heads, dk_heads, dv_heads = attention_backward(q_heads, k_heads, v_heads, d_o_heads, log_sum, 0)
        dq_local = lax.all_to_all(dq_heads, 'sp', 1, 2, tiled=True)
        dk_local = lax.all_to_all(dk_heads.astype(jnp.bfloat16), 'sp', 1, 2, tiled=True)
        dv_local = lax.all_to_all(dv_heads.astype(jnp.bfloat16), 'sp', 1, 2, tiled=True)
        if spread > 1:
            dk_local = dk_local.reshape(batch, seq_loc, num_kv, spread, head_dim).sum(axis=3, dtype=jnp.float32).astype(jnp.bfloat16)
            dv_local = dv_local.reshape(batch, seq_loc, num_kv, spread, head_dim).sum(axis=3, dtype=jnp.float32).astype(jnp.bfloat16)
        dq_lin = rotate_back(dq_local, cos_t, sin_t).astype(jnp.bfloat16)
        dk_lin = rotate_back(dk_local, cos_t, sin_t).astype(jnp.bfloat16)
        d_normed = project_back(dq_lin, dk_lin, dv_local, w_q, w_k, w_v)
        d_wq = jnp.einsum('bsd,bshe->dhe', normed, dq_lin, preferred_element_type=jnp.float32)
        d_wk = jnp.einsum('bsd,bshe->dhe', normed, dk_lin, preferred_element_type=jnp.float32)
        d_wv = jnp.einsum('bsd,bshe->dhe', normed, dv_local, preferred_element_type=jnp.float32)
        d_x_norm = norm_backward(d_normed, x_hat, inv_rms, gain)
        d_gain = jnp.sum(d_normed * x_hat, axis=(0, 1))
        d_x = (dy_local.astype(jnp.float32) + d_x_norm).astype(jnp.bfloat16)
        d_wq, d_wk, d_wv, d_wo, d_gain = lax.psum((d_wq, d_wk, d_wv, d_wo, d_gain), 'sp')
        return y_out, d_x, d_wq, d_wk, d_wv, d_wo, d_gain

    specs_in = (P('dp', 'sp', None), P('dp', 'sp', None), P(None), P(None, None, None), P(None, None, None), P(None, None, None), P(None, None, None))
    specs_out = (P('dp', 'sp', None), P('dp', 'sp', None), P('dp', None, None), P('dp', None, None), P('dp', None, None), P('dp', None, None), P('dp'))
    return jax.shard_map(local_step, mesh=mesh, in_specs=specs_in, out_specs=specs_out, check_vma=False)
```

profile of v0, /device:TPU:81, one launch (start us, length us, event | category | flops | bytes accessed | tf_op | source)
XLA Modules:
  0.0 1300.7 jit_solution(16884036137960751665)
XLA Ops:
  101.2 215.6 %while.28 = (s32[]{:T(128)}, bf16[3,1,1024,1,4,64]{2,5,4,3,1,0:T(8,128)(2,1)}, f32[3,1,1,4,1024,1]{4,3,5,2,1,0:T(4,128)S(1)}, s32[3]{0:T(128)S(1)}, bf16[1,3072,...) while((s32[]{:T(128)}, ...), condition=%wide.region_4.5_spmd.clone, body=%wide.region_1.4_spmd.clone.sunk | while | flops 3375625216 | bytes 165552336 | solution.py:88
  106.6 22.1 %fusion.143 = (f32[4,1024]{1,0:T(4,128)S(1)}, f32[1024,4,3072]{2,0,1:T(8,128)}) fusion(pred[1024,3072]{1,0:T(8,128)(4,1)} %iota_compare_fusion.4, bf16[1,3072,1,64]{1,3,2,0:T(8,128)(2,1)} %get-tuple-element.359, bf16[1,3072,1,4,64]{1,4,3,2,0:T(8,128)(2,1)} %get-tuple-element.358, s32[]{:T(128)S(6)} %select_n.47), kind=kOutput, calls=%fused_computation.6.clone.1 | convolution fusion | flops 1648357376 | bytes 54411268 | tf_op jit(solution)/shard_map/while/body/eval_jaxpr/bqkgd,btkd->bkgqt/dot_general | solution.py:78
  128.7 22.7 %fusion.144 = f32[4,1024]{1,0:T(4,128)S(1)} fusion(f32[1024,4,3072]{2,0,1:T(8,128)} %get-tuple-element.318, f32[4,1024]{1,0:T(4,128)S(1)} %get-tuple-element.319, pred[1024,3072]{1,0:T(8,128)(4,1)} %iota_compare_fusion.4), kind=kLoop, calls=%fused_computation.5.clone.1 | loop fusion | flops 50327552 | bytes 53510144 | tf_op jit(solution)/shard_map/while/body/eval_jaxpr/reduce_sum | solution.py:83
  151.4 21.6 %fusion.145 = bf16[3,1,1024,1,4,64]{2,5,4,3,1,0:T(8,128)(2,1)} fusion(bf16[3,1,1024,1,4,64]{2,5,4,3,1,0:T(8,128)(2,1)} %get-tuple-element.344, s32[]{:T(128)S(6)} %copy.69, f32[4,1024]{1,0:T(4,128)S(1)} %fusion.144, f32[4,1024]{1,0:T(4,128)S(1)} %get-tuple-element.319, f32[1024,4,3072]{2,0,1:T(8,128)} %get-tuple-element.318, ...), kind=kOutput, calls=%fused_computation.12.clone.1 | convolution fusion | flops 1673789440 | bytes 54427652 | tf_op jit(solution)/shard_map/while/body/eval_jaxpr/bkgqt,btkd->bqkgd/dot_general | solution.py:85
  178.5 22.1 %fusion.143 = (f32[4,1024]{1,0:T(4,128)S(1)}, f32[1024,4,3072]{2,0,1:T(8,128)}) fusion(pred[1024,3072]{1,0:T(8,128)(4,1)} %iota_compare_fusion.4, bf16[1,3072,1,64]{1,3,2,0:T(8,128)(2,1)} %get-tuple-element.359, bf16[1,3072,1,4,64]{1,4,3,2,0:T(8,128)(2,1)} %get-tuple-element.358, s32[]{:T(128)S(6)} %select_n.47), kind=kOutput, calls=%fused_computation.6.clone.1 | convolution fusion | flops 1648357376 | bytes 54411268 | tf_op jit(solution)/shard_map/while/body/eval_jaxpr/bqkgd,btkd->bkgqt/dot_general | solution.py:78
  200.6 22.7 %fusion.144 = f32[4,1024]{1,0:T(4,128)S(1)} fusion(f32[1024,4,3072]{2,0,1:T(8,128)} %get-tuple-element.318, f32[4,1024]{1,0:T(4,128)S(1)} %get-tuple-element.319, pred[1024,3072]{1,0:T(8,128)(4,1)} %iota_compare_fusion.4), kind=kLoop, calls=%fused_computation.5.clone.1 | loop fusion | flops 50327552 | bytes 53510144 | tf_op jit(solution)/shard_map/while/body/eval_jaxpr/reduce_sum | solution.py:83
  223.3 21.6 %fusion.145 = bf16[3,1,1024,1,4,64]{2,5,4,3,1,0:T(8,128)(2,1)} fusion(bf16[3,1,1024,1,4,64]{2,5,4,3,1,0:T(8,128)(2,1)} %get-tuple-element.344, s32[]{:T(128)S(6)} %copy.69, f32[4,1024]{1,0:T(4,128)S(1)} %fusion.144, f32[4,1024]{1,0:T(4,128)S(1)} %get-tuple-element.319, f32[1024,4,3072]{2,0,1:T(8,128)} %get-tuple-element.318, ...), kind=kOutput, calls=%fused_computation.12.clone.1 | convolution fusion | flops 1673789440 | bytes 54427652 | tf_op jit(solution)/shard_map/while/body/eval_jaxpr/bkgqt,btkd->bqkgd/dot_general | solution.py:85
  250.3 22.1 %fusion.143 = (f32[4,1024]{1,0:T(4,128)S(1)}, f32[1024,4,3072]{2,0,1:T(8,128)}) fusion(pred[1024,3072]{1,0:T(8,128)(4,1)} %iota_compare_fusion.4, bf16[1,3072,1,64]{1,3,2,0:T(8,128)(2,1)} %get-tuple-element.359, bf16[1,3072,1,4,64]{1,4,3,2,0:T(8,128)(2,1)} %get-tuple-element.358, s32[]{:T(128)S(6)} %select_n.47), kind=kOutput, calls=%fused_computation.6.clone.1 | convolution fusion | flops 1648357376 | bytes 54411268 | tf_op jit(solution)/shard_map/while/body/eval_jaxpr/bqkgd,btkd->bkgqt/dot_general | solution.py:78
  272.5 22.7 %fusion.144 = f32[4,1024]{1,0:T(4,128)S(1)} fusion(f32[1024,4,3072]{2,0,1:T(8,128)} %get-tuple-element.318, f32[4,1024]{1,0:T(4,128)S(1)} %get-tuple-element.319, pred[1024,3072]{1,0:T(8,128)(4,1)} %iota_compare_fusion.4), kind=kLoop, calls=%fused_computation.5.clone.1 | loop fusion | flops 50327552 | bytes 53510144 | tf_op jit(solution)/shard_map/while/body/eval_jaxpr/reduce_sum | solution.py:83
  295.2 21.6 %fusion.145 = bf16[3,1,1024,1,4,64]{2,5,4,3,1,0:T(8,128)(2,1)} fusion(bf16[3,1,1024,1,4,64]{2,5,4,3,1,0:T(8,128)(2,1)} %get-tuple-element.344, s32[]{:T(128)S(6)} %copy.69, f32[4,1024]{1,0:T(4,128)S(1)} %fusion.144, f32[4,1024]{1,0:T(4,128)S(1)} %get-tuple-element.319, f32[1024,4,3072]{2,0,1:T(8,128)} %get-tuple-element.318, ...), kind=kOutput, calls=%fused_computation.12.clone.1 | convolution fusion | flops 1673789440 | bytes 54427652 | tf_op jit(solution)/shard_map/while/body/eval_jaxpr/bkgqt,btkd->bqkgd/dot_general | solution.py:85
  318.2 372.3 %while.29 = (s32[]{:T(128)}, f32[1,3072,1,64]{1,3,2,0:T(8,128)}, f32[1,3072,1,64]{1,3,2,0:T(8,128)S(1)}, bf16[3,1,1024,1,4,64]{2,5,4,3,1,0:T(8,128)(2,1)}, s32[3...) while((s32[]{:T(128)}, f32[1,3072,1,64]{1,3,2,0:T(8,128)}, ...), condition=%wide.region_7.8_spmd.clone, body=%wide.region_5.7_spmd.clone.sunk | while | flops 8220832768 | bytes 324755776 | solution.py:122
  337.0 31.2 %fusion.154 = (f32[4,1024]{1,0:T(4,128)S(1)}, f32[1,1,4,1024,3072]{4,3,2,1,0:T(8,128)}) fusion(bf16[1024,4,3072]{2,0,1:T(8,128)(2,1)} %convolution_convert_fusion.4, f32[4,1024]{1,0:T(4,128)S(1)} %dynamic-slice_bitcast_fusion.2, bf16[1,3072,1,64]{1,3,2,0:T(8,128)(2,1)S(1)} %copy-done.9, bf16[1,3072,1,4,64]{1,4,3,2,0:T(8,128)(2,1)} %get-tuple-element.398, ...), kind=kOutput, calls=%fused_computation.28.clone.1 | convolution fusion | flops 1686106112 | bytes 79593472 | tf_op jit(solution)/shard_map/while/body/eval_jaxpr/bqkgd,btkd->bkgqt/dot_general | solution.py:109
  368.2 32.6 %fusion.155 = bf16[4,1024,3072]{2,1,0:T(8,128)(2,1)} fusion(f32[1,1,4,1024,3072]{4,3,2,1,0:T(8,128)} %get-tuple-element.330, bf16[1024,4,3072]{2,0,1:T(8,128)(2,1)} %convolution_convert_fusion.4, f32[4,1024]{1,0:T(4,128)S(1)} %get-tuple-element.331), kind=kLoop, calls=%fused_computation.32.clone.1 | loop fusion | flops 62914560 | bytes 100679680 | tf_op jit(solution)/shard_map/reshape.27
  400.9 17.4 %fusion.157 = f32[1,3072,1,64]{1,3,2,0:T(8,128)S(1)} fusion(f32[1,1,4,1024,3072]{4,3,2,1,0:T(8,128)} %get-tuple-element.330, f32[1,3072,1,64]{1,3,2,0:T(8,128)S(1)} %get-tuple-element.381, bf16[1,3072,1,4,64]{1,4,3,2,0:T(8,128)(2,1)} %get-tuple-element.401, s32[]{:T(128)S(6)} %select_n.48, pred[]{:T(512)S(6)} %compare.3), kind=kOutput, calls=%fused_computation.41.clone.1 | convolution fusion | flops 1623588864 | bytes 52428804 | tf_op jit(solution)/shard_map/while/body/eval_jaxpr/bkgqt,bqkgd->btkd/dot_general | solution.py:118
  460.9 31.3 %fusion.154 = (f32[4,1024]{1,0:T(4,128)S(1)}, f32[1,1,4,1024,3072]{4,3,2,1,0:T(8,128)}) fusion(bf16[1024,4,3072]{2,0,1:T(8,128)(2,1)} %convolution_convert_fusion.4, f32[4,1024]{1,0:T(4,128)S(1)} %dynamic-slice_bitcast_fusion.2, bf16[1,3072,1,64]{1,3,2,0:T(8,128)(2,1)S(1)} %copy-done.9, bf16[1,3072,1,4,64]{1,4,3,2,0:T(8,128)(2,1)} %get-tuple-element.398, ...), kind=kOutput, calls=%fused_computation.28.clone.1 | convolution fusion | flops 1686106112 | bytes 79593472 | tf_op jit(solution)/shard_map/while/body/eval_jaxpr/bqkgd,btkd->bkgqt/dot_general | solution.py:109
  492.1 32.6 %fusion.155 = bf16[4,1024,3072]{2,1,0:T(8,128)(2,1)} fusion(f32[1,1,4,1024,3072]{4,3,2,1,0:T(8,128)} %get-tuple-element.330, bf16[1024,4,3072]{2,0,1:T(8,128)(2,1)} %convolution_convert_fusion.4, f32[4,1024]{1,0:T(4,128)S(1)} %get-tuple-element.331), kind=kLoop, calls=%fused_computation.32.clone.1 | loop fusion | flops 62914560 | bytes 100679680 | tf_op jit(solution)/shard_map/reshape.27
  524.8 17.4 %fusion.157 = f32[1,3072,1,64]{1,3,2,0:T(8,128)S(1)} fusion(f32[1,1,4,1024,3072]{4,3,2,1,0:T(8,128)} %get-tuple-element.330, f32[1,3072,1,64]{1,3,2,0:T(8,128)S(1)} %get-tuple-element.381, bf16[1,3072,1,4,64]{1,4,3,2,0:T(8,128)(2,1)} %get-tuple-element.401, s32[]{:T(128)S(6)} %select_n.48, pred[]{:T(512)S(6)} %compare.3), kind=kOutput, calls=%fused_computation.41.clone.1 | convolution fusion | flops 1623588864 | bytes 52428804 | tf_op jit(solution)/shard_map/while/body/eval_jaxpr/bkgqt,bqkgd->btkd/dot_general | solution.py:118
  584.8 31.3 %fusion.154 = (f32[4,1024]{1,0:T(4,128)S(1)}, f32[1,1,4,1024,3072]{4,3,2,1,0:T(8,128)}) fusion(bf16[1024,4,3072]{2,0,1:T(8,128)(2,1)} %convolution_convert_fusion.4, f32[4,1024]{1,0:T(4,128)S(1)} %dynamic-slice_bitcast_fusion.2, bf16[1,3072,1,64]{1,3,2,0:T(8,128)(2,1)S(1)} %copy-done.9, bf16[1,3072,1,4,64]{1,4,3,2,0:T(8,128)(2,1)} %get-tuple-element.398, ...), kind=kOutput, calls=%fused_computation.28.clone.1 | convolution fusion | flops 1686106112 | bytes 79593472 | tf_op jit(solution)/shard_map/while/body/eval_jaxpr/bqkgd,btkd->bkgqt/dot_general | solution.py:109
  616.1 32.6 %fusion.155 = bf16[4,1024,3072]{2,1,0:T(8,128)(2,1)} fusion(f32[1,1,4,1024,3072]{4,3,2,1,0:T(8,128)} %get-tuple-element.330, bf16[1024,4,3072]{2,0,1:T(8,128)(2,1)} %convolution_convert_fusion.4, f32[4,1024]{1,0:T(4,128)S(1)} %get-tuple-element.331), kind=kLoop, calls=%fused_computation.32.clone.1 | loop fusion | flops 62914560 | bytes 100679680 | tf_op jit(solution)/shard_map/reshape.27
  648.7 17.4 %fusion.157 = f32[1,3072,1,64]{1,3,2,0:T(8,128)S(1)} fusion(f32[1,1,4,1024,3072]{4,3,2,1,0:T(8,128)} %get-tuple-element.330, f32[1,3072,1,64]{1,3,2,0:T(8,128)S(1)} %get-tuple-element.381, bf16[1,3072,1,4,64]{1,4,3,2,0:T(8,128)(2,1)} %get-tuple-element.401, s32[]{:T(128)S(6)} %select_n.48, pred[]{:T(512)S(6)} %compare.3), kind=kOutput, calls=%fused_computation.41.clone.1 | convolution fusion | flops 1623588864 | bytes 52428804 | tf_op jit(solution)/shard_map/while/body/eval_jaxpr/bkgqt,bqkgd->btkd/dot_general | solution.py:118
  694.0 18.8 %reduce.5 = bf16[3072,64]{1,0:T(8,128)(2,1)} reduce(bf16[3072,1,1,64]{3,2,1,0:T(2,128)(2,1)} %bitcast.379, bf16[]{:T(256)} %broadcast.155), dimensions={1,2}, to_apply=%bitcast.279.reduce_sub_computation | reduce | bytes 786434
  724.9 17.9 %reduce.6 = bf16[3072,64]{1,0:T(8,128)(2,1)S(1)} reduce(bf16[3072,1,1,64]{3,2,1,0:T(2,128)(2,1)} %bitcast.380, bf16[]{:T(256)} %broadcast.155), dimensions={1,2}, to_apply=%bitcast.283.reduce_sub_computation | reduce | bytes 786434
  888.5 376.7 %all-reduce.3.cloned.1.call-done = (f32[2048,32,64]{0,2,1:T(8,128)}, f32[2048,8,64]{0,2,1:T(8,128)}, f32[2048,8,64]{0,2,1:T(8,128)}, f32[32,64,2048]{2,1,0:T(8,128)}) async-done(((f32[2048,32,64]{0,2,1:T(8,128)}, f32[2048,8,64]{0,2,1:T(8,128)}, f32[2048,8,64]{0,2,1:T(8,128)}, f32[32,64,2048]{2,1,0:T(8,128)}), (f32[2048,32,64]{0,2,1:T(8,128)}, f32[2048,8,64]{0,2,1:T(8,128)}, f32[2048,8,64]{0,2,1:T(8,128)}, ...) | async-done | bytes 41943056 | tf_op jit(solution)/shard_map/psum | solution.py:168
  1265.2 13.6 %copy.91 = f32[2048,32,64]{0,2,1:T(8,128)} copy(f32[2048,32,64]{0,2,1:T(8,128)} %get-tuple-element.409) | data formatting | bytes 33554432
  (211 shorter events, 410.6 us)
Async XLA Ops:
  9.1 37.0 %copy-start.31 = (f32[384]{0:T(512)}, f32[384]{0:T(512)S(1)}, u32[]{:S(2)}) copy-start(f32[384]{0:T(512)S(1)} %add_rsqrt_fusion) | copy-start | bytes 4612
  13.4 13.6 %all-to-all-start.2 = ((bf16[1,384,8,64]{1,3,0,2:T(8,128)(2,1)}), bf16[1,384,8,64]{1,3,0,2:T(8,128)(2,1)S(1)}, u32[]{:S(2)}, u32[]{:S(2)}) async-start(bf16[1,384,8,64]{1,3,0,2:T(8,128)(2,1)} %convert_bitcast_fusion.1), calls=%async_computation.2 | async-start | bytes 786432 | tf_op jit(solution)/shard_map/all_to_all | solution.py:144
  22.5 31.3 %copy-start.21 = (f32[384,32]{0,1:T(8,128)}, f32[384,32]{0,1:T(8,128)S(1)}, u32[]{:S(2)}) copy-start(f32[384,32]{0,1:T(8,128)S(1)} %get-tuple-element.217) | copy-start | bytes 147460
  22.5 31.3 %copy-start.23 = (f32[384,32]{0,1:T(8,128)}, f32[384,32]{0,1:T(8,128)S(1)}, u32[]{:S(2)}) copy-start(f32[384,32]{0,1:T(8,128)S(1)} %get-tuple-element.218) | copy-start | bytes 147460
  27.0 14.3 %all-to-all-start.1 = ((bf16[1,384,8,64]{1,3,0,2:T(8,128)(2,1)}), bf16[1,384,8,64]{1,3,0,2:T(8,128)(2,1)S(1)}, u32[]{:S(2)}, u32[]{:S(2)}) async-start(bf16[1,384,8,64]{1,3,0,2:T(8,128)(2,1)} %maximum_bitcast_fusion.1), calls=%async_computation.1 | async-start | bytes 786432 | tf_op jit(solution)/shard_map/all_to_all | solution.py:143
  41.3 25.4 %all-to-all-start.4 = ((bf16[1,384,32,64]{1,3,0,2:T(8,128)(2,1)}), bf16[1,384,32,64]{1,3,0,2:T(8,128)(2,1)}, u32[]{:S(2)}, u32[]{:S(2)}) async-start(bf16[1,384,32,64]{1,3,0,2:T(8,128)(2,1)} %fusion.84), calls=%async_computation.4 | async-start | bytes 3145728 | tf_op jit(solution)/shard_map/all_to_all | solution.py:151
  66.6 26.1 %all-to-all-start = ((bf16[1,384,32,64]{1,3,0,2:T(8,128)(2,1)}), bf16[1,384,32,64]{1,3,0,2:T(8,128)(2,1)}, u32[]{:S(2)}, u32[]{:S(2)}) async-start(bf16[1,384,32,64]{1,3,0,2:T(8,128)(2,1)} %maximum_bitcast_fusion), calls=%async_computation | async-start | bytes 3145728 | tf_op jit(solution)/shard_map/all_to_all | solution.py:142
  101.2 217.0 %copy-start.5 = (f32[1,3072,1,64]{1,3,2,0:T(8,128)S(1)}, f32[1,3072,1,64]{1,3,2,0:T(8,128)}, u32[]{:S(2)}) copy-start(f32[1,3072,1,64]{1,3,2,0:T(8,128)} %custom-call.1) | copy-start | bytes 2359300
  400.9 17.4 %copy-start.6 = (f32[1,3072,1,64]{1,3,2,0:T(8,128)S(1)}, f32[1,3072,1,64]{1,3,2,0:T(8,128)}, u32[]{:S(2)}) copy-start(f32[1,3072,1,64]{1,3,2,0:T(8,128)} %get-tuple-element.380) | copy-start | bytes 2359300 | tf_op jit(solution)/shard_map/while
  429.0 13.5 %copy-start.7 = (f32[1,3072,1,64]{1,3,2,0:T(8,128)}, f32[1,3072,1,64]{1,3,2,0:T(8,128)S(1)}, u32[]{:S(2)}) copy-start(f32[1,3072,1,64]{1,3,2,0:T(8,128)S(1)} %fusion.156) | copy-start | bytes 2359300 | tf_op jit(solution)/shard_map/while
  524.8 17.4 %copy-start.6 = (f32[1,3072,1,64]{1,3,2,0:T(8,128)S(1)}, f32[1,3072,1,64]{1,3,2,0:T(8,128)}, u32[]{:S(2)}) copy-start(f32[1,3072,1,64]{1,3,2,0:T(8,128)} %get-tuple-element.380) | copy-start | bytes 2359300 | tf_op jit(solution)/shard_map/while
  552.9 13.5 %copy-start.7 = (f32[1,3072,1,64]{1,3,2,0:T(8,128)}, f32[1,3072,1,64]{1,3,2,0:T(8,128)S(1)}, u32[]{:S(2)}) copy-start(f32[1,3072,1,64]{1,3,2,0:T(8,128)S(1)} %fusion.156) | copy-start | bytes 2359300 | tf_op jit(solution)/shard_map/while
  648.7 17.4 %copy-start.6 = (f32[1,3072,1,64]{1,3,2,0:T(8,128)S(1)}, f32[1,3072,1,64]{1,3,2,0:T(8,128)}, u32[]{:S(2)}) copy-start(f32[1,3072,1,64]{1,3,2,0:T(8,128)} %get-tuple-element.380) | copy-start | bytes 2359300 | tf_op jit(solution)/shard_map/while
  676.8 13.5 %copy-start.7 = (f32[1,3072,1,64]{1,3,2,0:T(8,128)}, f32[1,3072,1,64]{1,3,2,0:T(8,128)S(1)}, u32[]{:S(2)}) copy-start(f32[1,3072,1,64]{1,3,2,0:T(8,128)S(1)} %fusion.156) | copy-start | bytes 2359300 | tf_op jit(solution)/shard_map/while
  690.5 29.4 %copy-start.8 = (f32[1,3072,1,64]{1,3,2,0:T(8,128)S(1)}, f32[1,3072,1,64]{1,3,2,0:T(8,128)}, u32[]{:S(2)}) copy-start(f32[1,3072,1,64]{1,3,2,0:T(8,128)} %get-tuple-element.112) | copy-start | bytes 2359300
  715.5 28.6 %all-to-all-start.7 = ((bf16[8,2,12288]{2,1,0:T(2,128)(2,1)}), bf16[8,2,12288]{2,1,0:T(2,128)(2,1)S(1)}, u32[]{:S(2)}, u32[]{:S(2)}) async-start(bf16[8,2,12288]{2,1,0:T(2,128)(2,1)} %reshape.398), calls=%async_computation.7 | async-start | bytes 786432 | tf_op jit(solution)/shard_map/all_to_all | solution.py:155
  744.1 17.3 %all-to-all-start.6 = ((bf16[8,2,12288]{2,1,0:T(2,128)(2,1)}), bf16[8,2,12288]{2,1,0:T(2,128)(2,1)S(1)}, u32[]{:S(2)}, u32[]{:S(2)}) async-start(bf16[8,2,12288]{2,1,0:T(2,128)(2,1)} %reshape.402), calls=%async_computation.6 | async-start | bytes 786432 | tf_op jit(solution)/shard_map/all_to_all | solution.py:154
  761.4 28.3 %all-to-all-start.5 = ((bf16[8,2,49152]{2,1,0:T(2,128)(2,1)}), bf16[8,2,49152]{2,1,0:T(2,128)(2,1)}, u32[]{:S(2)}, u32[]{:S(2)}) async-start(bf16[8,2,49152]{2,1,0:T(2,128)(2,1)} %reshape.400), calls=%async_computation.5 | async-start | bytes 3145728 | tf_op jit(solution)/shard_map/all_to_all | solution.py:153
  789.7 28.4 %all-to-all-start.3 = ((bf16[8,2,49152]{2,1,0:T(2,128)(2,1)}), bf16[8,2,49152]{2,1,0:T(2,128)(2,1)}, u32[]{:S(2)}, u32[]{:S(2)}) async-start(bf16[8,2,49152]{2,1,0:T(2,128)(2,1)} %reshape.396), calls=%async_computation.3 | async-start | bytes 3145728 | tf_op jit(solution)/shard_map/all_to_all | solution.py:146
  794.7 470.5 %all-reduce.3.cloned.1.call-start = ((), (), s32[]{:S(2)}) async-start(), calls=%async_computation.8 | async-start | bytes 83886080 | tf_op jit(solution)/shard_map/psum | solution.py:168
  1265.2 13.6 %copy-start.15 = (f32[2048,8,64]{0,2,1:T(8,128)S(1)}, f32[2048,8,64]{0,2,1:T(8,128)}, u32[]{:S(2)}) copy-start(f32[2048,8,64]{0,2,1:T(8,128)} %get-tuple-element.410) | copy-start | bytes 12582916
  1265.2 20.3 %slice-start = ((s8[16777216]{0:T(1024)(128)(4,1)}), s8[4194304]{0:T(1024)(128)(4,1)S(1)}, s32[]{:S(2)}) async-start(s8[16777216]{0:T(1024)(128)(4,1)} %bitcast.367), calls=%async_computation.9 | async-start | bytes 8388608
  1265.2 20.3 %slice-start.1 = ((s8[16777216]{0:T(1024)(128)(4,1)}), s8[4194304]{0:T(1024)(128)(4,1)S(1)}, s32[]{:S(2)}) async-start(s8[16777216]{0:T(1024)(128)(4,1)} %bitcast.367), calls=%async_computation.10 | async-start | bytes 8388608
  1265.2 20.3 %slice-start.2 = ((s8[16777216]{0:T(1024)(128)(4,1)}), s8[4194304]{0:T(1024)(128)(4,1)S(1)}, s32[]{:S(2)}) async-start(s8[16777216]{0:T(1024)(128)(4,1)} %bitcast.367), calls=%async_computation.11 | async-start | bytes 8388608
  (30 other events, 208.3 us)
Sparse Core Ops, SparseCore 0:
  849.2 415.9 all-reduce.2
where the time goes:
time: 1320 us; the launch traced here: 1300 us
  matrix products  457 us (35%)
  waiting for transfers between devices  404 us (31%)
  other arithmetic  241 us (18%)
  local copies, waits for them, and re-layouts  125 us (9%)
  starting transfers between devices  40.3 us (3%)
  between operations  15 us (1%)
  blocking collectives  13.5 us (1%)
    psum x1, waiting for transfers between devices, local_step(): lax.psum((d_wq, d_wk, d_wv, d_wo, d_gain), 'sp')  377 us
    dot_general x6, matrix products, one_block(): jnp.einsum('bqkgd,btkd->bkgqt', q_rows, k_heads, preferred_element_type=j...  160 us
    another operation x5, other arithmetic  98.5 us
    reduce_sum x3, other arithmetic, one_block(): row_sum = jnp.sum(exp_scores, axis=-1, keepdims=True)  68.2 us
    unnamed x81, local copies, waits for them, and re-layouts  67.8 us
    dot_general x3, matrix products, one_block(): jnp.einsum('bkgqt,btkd->bqkgd', attn_weights, v_heads, preferred_element_...  64.8 us
    dot_general x3, matrix products, one_block(): jnp.einsum('bkgqt,bqkgd->btkd', attn_weights.astype(jnp.bfloat16), d_rows...  52.3 us
    dot_general x3, matrix products, one_block(): jnp.einsum('bkgqt,btkd->bqkgd', d_scores, k_heads, preferred_element_type...  40.4 us
  transfers between devices with their start and end apart: 9, of which 4 were waited for; matrix products, arithmetic and copies ran while one was open for 11% of the time, Pallas kernels for 0%

commit v1 on v0

v1 whole, which is shorter than its diff:
```python
import functools
import math
import jax
import jax.numpy as jnp
from jax import lax
from jax.experimental import pallas as pl
from jax.experimental.pallas import tpu as pltpu
from jax.sharding import PartitionSpec as P

ROPE_BASE = 1000000.0
NORM_EPS = 1e-5
LOG2E = math.log2(math.e)
BQ = 256
BK = 256
NT = (((1,), (1,)), ((), ()))
TN = (((0,), (0,)), ((), ()))
F32 = jnp.float32
BF16 = jnp.bfloat16


def rope_tables(positions, head_dim):
    half = head_dim // 2
    inv_freq = ROPE_BASE ** (-2.0 * jnp.arange(half, dtype=F32) / head_dim)
    angle = inv_freq[:, None] * positions[None, :]
    return jnp.cos(angle), jnp.sin(angle)


def rotate(vals, cos_t, sin_t):
    half = vals.shape[-2] // 2
    first = vals[..., :half, :]
    second = vals[..., half:, :]
    return jnp.concatenate([first * cos_t - second * sin_t, second * cos_t + first * sin_t], axis=-2)


def rotate_back(vals, cos_t, sin_t):
    half = vals.shape[-2] // 2
    first = vals[..., :half, :]
    second = vals[..., half:, :]
    return jnp.concatenate([first * cos_t + second * sin_t, second * cos_t - first * sin_t], axis=-2)


def norm_forward(x_local, gain):
    x_f32 = x_local.astype(F32)
    inv_rms = lax.rsqrt(jnp.mean(x_f32 * x_f32, axis=-1, keepdims=True) + NORM_EPS)
    x_hat = x_f32 * inv_rms
    return x_hat, inv_rms, (x_hat * gain).astype(BF16)


def dot(a, b):
    return jnp.dot(a, b, preferred_element_type=F32)


def dot_nt(a, b):
    return lax.dot_general(a, b, NT, preferred_element_type=F32)


def heads_cat(ref, num):
    dim = ref.shape[0] // num
    return jnp.concatenate([ref[h * dim:(h + 1) * dim, :] for h in range(num)], axis=1)


class RingGather:
    def __init__(self, seq_par, own, place, send_sem, recv_sem):
        me = lax.axis_index('sp')
        self.me = me
        self.partner = me + 1 - 2 * lax.rem(me, 2)
        self.right = lax.rem(me + 2, seq_par)
        self.left = lax.rem(me + seq_par - 2, seq_par)
        self.far = lax.rem(me + 4, seq_par)
        self.other = lambda b: b + 1 - 2 * lax.rem(b, 2)
        both = slice(None)

        def remote(num, src, dst, to):
            return pltpu.make_async_remote_copy(src_ref=src, dst_ref=dst, send_sem=send_sem.at[num], recv_sem=recv_sem.at[num], device_id={'sp': to}, device_id_type=pl.DeviceIdType.MESH)

        self.r1 = remote(0, own(0), place(me, 0), self.right)
        self.l1 = remote(1, own(1), place(me, 1), self.left)
        self.r2 = remote(2, own(1), place(me, 1), self.right)
        self.l2 = remote(3, own(0), place(me, 0), self.left)
        self.p0 = remote(4, own(both), place(me, both), self.partner)
        self.r3 = remote(5, place(self.left, 0), place(self.left, 0), self.right)
        self.l3 = remote(6, place(self.right, 1), place(self.right, 1), self.left)
        self.p1 = remote(7, place(self.left, both), place(self.left, both), self.partner)
        self.p2 = remote(8, place(self.right, both), place(self.right, both), self.partner)
        self.p3 = remote(9, place(self.far, both), place(self.far, both), self.partner)

    def start(self):
        self.r1.start()
        self.l1.start()
        self.r2.start()
        self.l2.start()
        self.p0.start()

    def forward(self):
        self.r1.wait_recv()
        self.r3.start()
        self.l1.wait_recv()
        self.l3.start()

    def relay_near(self):
        self.r2.wait_recv()
        self.p1.start()
        self.l2.wait_recv()
        self.p2.start()

    def relay_far(self):
        self.r3.wait_recv()
        self.l3.wait_recv()
        self.p3.start()

    def finish_sends(self):
        for copy in (self.r1, self.l1, self.r2, self.l2, self.p0, self.r3, self.l3, self.p1, self.p2, self.p3):
            copy.wait_send()

    def finish_recvs(self):
        for copy in (self.p0, self.p1, self.p2, self.p3):
            copy.wait_recv()


GATHER_SEMS = [pltpu.SemaphoreType.DMA((10,)), pltpu.SemaphoreType.DMA((10,))]


def greet(seq_par):
    me = lax.axis_index('sp')
    barrier = pltpu.get_barrier_semaphore()
    for peer in (me + 1 - 2 * lax.rem(me, 2), lax.rem(me + 2, seq_par), lax.rem(me + seq_par - 2, seq_par)):
        pl.semaphore_signal(barrier, inc=1, device_id={'sp': peer}, device_id_type=pl.DeviceIdType.MESH)
    pl.semaphore_wait(barrier, 3)


def row_place(ref, rows):
    half = rows // 2

    def place(block, part):
        if isinstance(part, int):
            return ref.at[pl.ds(pl.multiple_of(block * rows + part * half, half), half), :]
        return ref.at[pl.ds(pl.multiple_of(block * rows, rows), rows), :]

    return place


def row_own(ref, rows):
    half = rows // 2

    def own(part):
        if isinstance(part, int):
            return ref.at[part * half:(part + 1) * half, :]
        return ref

    return own


class Bounce:
    def __init__(self, own, buffer, place, sems):
        self.fetch = pltpu.make_async_copy(own, buffer, sems.at[0])
        self.keep = pltpu.make_async_copy(buffer, place, sems.at[1])

    def turn(self):
        self.fetch.wait()
        self.keep.start()


def at_step(step):
    return pl.when(pl.program_id(0) == step)


def project_kernel(seq_par, group, own_ref, w_ref, cos_ref, sin_ref, all_ref, q_ref, k_ref, v_ref, tile, bounce, tile_sem, bounce_sem, send_sem, recv_sem):
    rows = own_ref.shape[0]
    dim = k_ref.shape[0]
    greet(seq_par)
    block_of = row_place(all_ref, rows)
    ring = RingGather(seq_par, row_own(own_ref, rows), block_of, send_sem, recv_sem)
    ring.start()

    def project(rows_ref, block):
        cols = pl.ds(pl.multiple_of(block * rows, rows), rows)
        cos_t = cos_ref[:, cols]
        sin_t = sin_ref[:, cols]
        lin = dot_nt(w_ref[...], rows_ref[...])
        for h in range(group + 2):
            part = lin[h * dim:(h + 1) * dim, :]
            if h < group:
                q_ref[h * dim:(h + 1) * dim, cols] = rotate(part, cos_t, sin_t).astype(BF16)
            elif h == group:
                k_ref[:, cols] = rotate(part, cos_t, sin_t).astype(BF16)
            else:
                v_ref[:, cols] = part.astype(BF16)

    def gathered(block):
        copy = pltpu.make_async_copy(block_of(block, slice(None)), tile, tile_sem)
        copy.start()
        copy.wait()
        project(tile, block)

    fetch = pltpu.make_async_copy(own_ref, bounce, bounce_sem)
    fetch.start()
    fetch.wait()
    keep = pltpu.make_async_copy(bounce, block_of(ring.me, slice(None)), bounce_sem)
    keep.start()
    project(bounce, ring.me)
    ring.p0.wait_recv()
    gathered(ring.partner)
    ring.forward()
    ring.relay_near()
    gathered(ring.left)
    gathered(ring.right)
    ring.p1.wait_recv()
    gathered(ring.other(ring.left))
    ring.p2.wait_recv()
    gathered(ring.other(ring.right))
    ring.relay_far()
    gathered(ring.far)
    ring.p3.wait_recv()
    gathered(ring.other(ring.far))
    keep.wait()
    ring.finish_sends()


def gather_project(normed, w_own, cos_t, sin_t, group, seq_par):
    rows, d_model = normed.shape
    dim = w_own.shape[0] // (group + 2)
    seq = rows * seq_par
    vmem = pl.BlockSpec(memory_space=pltpu.VMEM)
    hbm = pl.BlockSpec(memory_space=pl.ANY)
    return pl.pallas_call(
        functools.partial(project_kernel, seq_par, group),
        in_specs=[hbm, vmem, vmem, vmem],
        out_specs=[hbm, vmem, vmem, vmem],
        out_shape=[
            jax.ShapeDtypeStruct((seq, d_model), BF16),
            jax.ShapeDtypeStruct((group * dim, seq), BF16),
            jax.ShapeDtypeStruct((dim, seq), BF16),
            jax.ShapeDtypeStruct((dim, seq), BF16),
        ],
        scratch_shapes=[pltpu.VMEM((rows, d_model), BF16), pltpu.VMEM((rows, d_model), BF16), pltpu.SemaphoreType.DMA, pltpu.SemaphoreType.DMA] + GATHER_SEMS,
        compiler_params=pltpu.CompilerParams(collective_id=1, has_side_effects=True, vmem_limit_bytes=48 << 20),
        cost_estimate=pl.CostEstimate(flops=2 * seq * d_model * (group + 2) * dim, transcendentals=0, bytes_accessed=4 * seq * d_model),
        name='gather_project',
    )(normed, w_own, cos_t, sin_t)


def forward_kernel(seq_par, group, scale, q_ref, k_ref, v_ref, own_ref, o_ref, lse_ref, all_ref, bounce, bounce_sem, send_sem, recv_sem):
    block = pl.program_id(0)
    blocks = k_ref.shape[0] // BQ
    rows = own_ref.shape[0]
    place = row_place(all_ref, rows)
    ring = RingGather(seq_par, row_own(own_ref, rows), place, send_sem, recv_sem)
    local = Bounce(own_ref, bounce, place(ring.me, slice(None)), bounce_sem)

    @at_step(0)
    def _():
        greet(seq_par)
        ring.start()
        local.fetch.start()

    @at_step(1)
    def _():
        local.turn()

    @at_step(blocks * 7 // 12)
    def _():
        ring.forward()

    @at_step(blocks * 10 // 12)
    def _():
        ring.relay_near()

    dim = k_ref.shape[1]
    wide = group * BQ
    q_cat = heads_cat(q_ref, group)
    factor = scale * LOG2E

    def step(start, carry, masked):
        m_old, l_old, acc = carry
        keys = k_ref[pl.ds(start, BK), :]
        scores = dot(keys, q_cat) * factor
        if masked:
            row = lax.broadcasted_iota(jnp.int32, (BK, wide), 0)
            col = lax.broadcasted_iota(jnp.int32, (BK, wide), 1) % BQ
            scores = jnp.where(row <= col, scores, -1e30)
        m_new = jnp.maximum(m_old, jnp.max(scores, axis=0, keepdims=True))
        probs = jnp.exp2(scores - m_new)
        alpha = jnp.exp2(m_old - m_new)
        l_new = l_old * alpha + jnp.sum(probs, axis=0, keepdims=True)
        out = dot(v_ref[:, pl.ds(start, BK)], probs.astype(BF16))
        return m_new, l_new, acc * alpha + out

    init = (jnp.full((1, wide), -1e30, F32), jnp.zeros((1, wide), F32), jnp.zeros((dim, wide), F32))
    carry = lax.fori_loop(0, block, lambda i, c: step(pl.multiple_of(i * BK, BK), c, False), init)
    m_fin, l_fin, acc = step(pl.multiple_of(block * BK, BK), carry, True)
    out = (acc / l_fin).astype(BF16)
    lse = m_fin + jnp.log2(l_fin)
    for h in range(group):
        o_ref[h * dim:(h + 1) * dim, :] = out[:, h * BQ:(h + 1) * BQ]
        lse_ref[h:h + 1, :] = lse[:, h * BQ:(h + 1) * BQ]

    @at_step(blocks - 1)
    def _():
        ring.relay_far()
        local.keep.wait()
        ring.finish_recvs()
        ring.finish_sends()


def attention_forward(q_t, k_rows, v_t, d_out, group, seq_par):
    dim, seq = v_t.shape
    rows, d_model = d_out.shape
    scale = dim ** -0.5
    pairs = seq * (seq + BQ) // 2 * group
    hbm = pl.BlockSpec(memory_space=pl.ANY)
    return pl.pallas_call(
        functools.partial(forward_kernel, seq_par, group, scale),
        grid=(seq // BQ,),
        in_specs=[
            pl.BlockSpec((group * dim, BQ), lambda j: (0, j)),
            pl.BlockSpec((seq, dim), lambda j: (0, 0)),
            pl.BlockSpec((dim, seq), lambda j: (0, 0)),
            hbm,
        ],
        out_specs=[
            pl.BlockSpec((group * dim, BQ), lambda j: (0, j)),
            pl.BlockSpec((group, BQ), lambda j: (0, j)),
            hbm,
        ],
        out_shape=[
            jax.ShapeDtypeStruct((group * dim, seq), BF16),
            jax.ShapeDtypeStruct((group, seq), F32),
            jax.ShapeDtypeStruct((seq, d_model), BF16),
        ],
        scratch_shapes=[pltpu.VMEM((rows, d_model), BF16), pltpu.SemaphoreType.DMA((2,))] + GATHER_SEMS,
        compiler_params=pltpu.CompilerParams(collective_id=2, has_side_effects=True, vmem_limit_bytes=48 << 20),
        cost_estimate=pl.CostEstimate(flops=16 * pairs * dim, transcendentals=pairs, bytes_accessed=8 * group * dim * seq),
        name='attn_fwd',
    )(q_t, k_rows, v_t, d_out)


def backward_kernel(seq_par, group, scale, q_ref, dy_ref, wo_ref, o_ref, lse_ref, k_ref, v_ref, kt_ref, cos_ref, sin_ref, own_ref, dqb_ref, dk_ref, dv_ref, all_ref, dqa_ref, dk_acc, dv_acc, dq_buf, bounce, bounce_sem, send_sem, recv_sem, dqa_sem, dq_send, dq_recv):
    block = pl.program_id(0)
    blocks = k_ref.shape[0] // BQ
    dim = k_ref.shape[1]
    wide = group * BQ
    factor = scale * LOG2E
    rows = own_ref.shape[0]
    half = dqa_ref.shape[1]
    place = row_place(all_ref, rows)
    ring = RingGather(seq_par, row_own(own_ref, rows), place, send_sem, recv_sem)
    local = Bounce(own_ref, bounce, place(ring.me, slice(None)), bounce_sem)
    dq_place = row_place(dqa_ref, rows)
    dq_ring = RingGather(seq_par, lambda part: dq_place(ring.me, part), dq_place, dq_send, dq_recv)

    @at_step(0)
    def _():
        greet(seq_par)
        ring.start()
        local.fetch.start()
        dk_acc[...] = jnp.zeros_like(dk_acc)
        dv_acc[...] = jnp.zeros_like(dv_acc)

    @at_step(1)
    def _():
        local.turn()

    @at_step(blocks * 5 // 12)
    def _():
        ring.forward()

    @at_step(blocks * 8 // 12)
    def _():
        ring.relay_near()

    @at_step(blocks * 10 // 12)
    def _():
        ring.relay_far()
        store = pltpu.make_async_copy(dq_buf.at[:, :half], dq_place(ring.me, slice(None)), dqa_sem)
        store.start()
        store.wait()
        dq_ring.start()

    @at_step(blocks * 11 // 12)
    def _():
        dq_ring.forward()

    do_t = dot_nt(wo_ref[...], dy_ref[...]).astype(BF16)
    q_cat = heads_cat(q_ref, group)
    do_cat = jnp.concatenate([do_t[h * dim:(h + 1) * dim, :] for h in range(group)], axis=1)
    o_cat = heads_cat(o_ref, group)
    lse = jnp.concatenate([lse_ref[h:h + 1, :] for h in range(group)], axis=1)
    delta = jnp.sum(do_cat.astype(F32) * o_cat.astype(F32), axis=0, keepdims=True)

    def step(start, dq, masked):
        keys = pl.ds(start, BK)
        scores = dot(k_ref[keys, :], q_cat) * factor
        if masked:
            row = lax.broadcasted_iota(jnp.int32, (BK, wide), 0)
            col = lax.broadcasted_iota(jnp.int32, (BK, wide), 1) % BQ
            scores = jnp.where(row <= col, scores, -1e30)
        probs = jnp.exp2(scores - lse)
        d_probs = dot(v_ref[keys, :], do_cat).astype(BF16).astype(F32)
        d_scores = (probs * (d_probs - delta)).astype(BF16)
        dv_acc[:, keys] += dot_nt(do_cat, probs.astype(BF16))
        dk_acc[:, keys] += dot_nt(q_cat, d_scores)
        return dq + dot(kt_ref[:, keys], d_scores)

    dq = lax.fori_loop(0, block, lambda i, c: step(pl.multiple_of(i * BK, BK), c, False), jnp.zeros((dim, wide), F32))
    dq = step(pl.multiple_of(block * BK, BK), dq, True)
    dq = (dq * scale).astype(BF16).astype(F32)
    cols = pl.ds(pl.multiple_of(block * BQ, BQ), BQ)
    cos_t = cos_ref[:, cols]
    sin_t = sin_ref[:, cols]
    for h in range(group):
        dq_buf[h * dim:(h + 1) * dim, cols] = rotate_back(dq[:, h * BQ:(h + 1) * BQ], cos_t, sin_t).astype(BF16)

    @at_step(blocks - 1)
    def _():
        store = pltpu.make_async_copy(dq_buf.at[:, half:], dqb_ref, dqa_sem)
        store.start()
        dk = (dk_acc[...] * scale).astype(BF16).astype(F32)
        dk_ref[...] = rotate_back(dk, cos_ref[...], sin_ref[...]).astype(BF16)
        dv_ref[...] = dv_acc[...].astype(BF16)
        dq_ring.relay_near()
        ring.finish_recvs()
        ring.finish_sends()
        local.keep.wait()
        store.wait()
        dq_ring.relay_far()
        dq_ring.finish_recvs()
        dq_ring.finish_sends()


def attention_backward(q_t, dy_all, wo_own, o_t, lse, k_rows, v_rows, k_t, cos_t, sin_t, group, seq_par):
    dim, seq = k_t.shape
    rows, d_model = wo_own.shape
    scale = dim ** -0.5
    half = seq // 2
    pairs = seq * (seq + BQ) // 2 * group
    tile = pl.BlockSpec((rows, BQ), lambda j: (0, j))
    whole = lambda shape: pl.BlockSpec(shape, lambda j: (0, 0))
    hbm = pl.BlockSpec(memory_space=pl.ANY)
    return pl.pallas_call(
        functools.partial(backward_kernel, seq_par, group, scale),
        grid=(seq // BQ,),
        in_specs=[tile, pl.BlockSpec((BQ, d_model), lambda j: (j, 0)), whole(wo_own.shape), tile, pl.BlockSpec((group, BQ), lambda j: (0, j)), whole((seq, dim)), whole((seq, dim)), whole((dim, seq)), whole(cos_t.shape), whole(sin_t.shape), hbm],
        out_specs=[hbm, whole((dim, seq)), whole((dim, seq)), hbm, hbm],
        out_shape=[
            jax.ShapeDtypeStruct((rows, seq - half), BF16),
            jax.ShapeDtypeStruct((dim, seq), BF16),
            jax.ShapeDtypeStruct((dim, seq), BF16),
            jax.ShapeDtypeStruct((rows * seq_par, seq), BF16),
            jax.ShapeDtypeStruct((rows * seq_par, half), BF16),
        ],
        scratch_shapes=[pltpu.VMEM((dim, seq), F32), pltpu.VMEM((dim, seq), F32), pltpu.VMEM((rows, seq), BF16), pltpu.VMEM((rows, seq), BF16), pltpu.SemaphoreType.DMA((2,))] + GATHER_SEMS + [pltpu.SemaphoreType.DMA] + GATHER_SEMS,
        compiler_params=pltpu.CompilerParams(collective_id=3, has_side_effects=True, vmem_limit_bytes=56 << 20),
        cost_estimate=pl.CostEstimate(flops=40 * pairs * dim, transcendentals=pairs, bytes_accessed=12 * group * dim * seq),
        name='attn_bwd',
    )(q_t, dy_all, wo_own, o_t, lse, k_rows, v_rows, k_t, cos_t, sin_t, o_t)


def solution(mesh):
    seq_par = mesh.shape['sp']

    def local_step(x_local, dy_local, gain, w_q, w_k, w_v, w_o):
        _, seq_loc, d_model = x_local.shape
        num_q, dim = w_q.shape[1], w_q.shape[2]
        num_kv = w_k.shape[1]
        group = num_q // num_kv
        if num_kv != seq_par or seq_par % 4:
            raise ValueError('unsupported mesh')
        seq = seq_loc * seq_par
        index = lax.axis_index('sp')
        x_local = x_local[0]
        dy_local = dy_local[0]
        wq_t = jnp.transpose(w_q, (1, 2, 0)).reshape(num_q * dim, d_model)
        wk_t = jnp.transpose(w_k, (1, 2, 0)).reshape(num_kv * dim, d_model)
        wv_t = jnp.transpose(w_v, (1, 2, 0)).reshape(num_kv * dim, d_model)
        wo_t = w_o.reshape(num_q * dim, d_model)
        own_q = lambda w: lax.dynamic_slice_in_dim(w, index * group * dim, group * dim, 0)
        own_kv = lambda w: lax.dynamic_slice_in_dim(w, index * dim, dim, 0)
        gather = lambda a: lax.all_gather(a, 'sp', axis=0, tiled=True)

        cos_t, sin_t = rope_tables(jnp.arange(seq, dtype=F32), dim)
        x_hat, inv_rms, normed = norm_forward(x_local, gain)
        w_own = jnp.concatenate([own_q(wq_t), own_kv(wk_t), own_kv(wv_t)], axis=0)
        normed_all, q_t, k_t, v_t = gather_project(normed, w_own, cos_t, sin_t, group, seq_par)
        k_rows = k_t.T
        v_rows = v_t.T
        o_t, lse, dy_all = attention_forward(q_t, k_rows, v_t, dy_local, group, seq_par)
        dqb_t, dk_t, dv_t, o_all, dqa_all = attention_backward(q_t, dy_all, own_q(wo_t), o_t, lse, k_rows, v_rows, k_t, cos_t, sin_t, group, seq_par)
        dqb_all = gather(dqb_t)
        dk_all = gather(dk_t)
        dv_all = gather(dv_t)
        half = seq // 2
        at_col = lambda a, start: lax.dynamic_slice_in_dim(a, start, seq_loc, 1)
        mine = lambda a: at_col(a, index * seq_loc)
        back = lambda a, w: lax.dot_general(a, w, TN, preferred_element_type=F32)
        low = index * seq_loc < half
        dq_mine = jnp.where(low, at_col(dqa_all, jnp.where(low, index * seq_loc, 0)), at_col(dqb_all, jnp.where(low, 0, index * seq_loc - half)))
        y_out = (x_local.astype(F32) + back(mine(o_all), wo_t)).astype(BF16)
        d_wo = dot(o_all, dy_all)
        d_wqa = dot(dqa_all, normed_all[:half])
        d_wqa, dqb_all = lax.optimization_barrier((d_wqa, dqb_all))
        d_wq = d_wqa + dot(dqb_all, normed_all[half:])
        d_wk = dot(dk_all, normed_all)
        d_wv = dot(dv_all, normed_all)
        d_normed = (back(dq_mine, wq_t) + back(mine(dk_all), wk_t) + back(mine(dv_all), wv_t)).astype(BF16).astype(F32)
        d_gain = lax.psum(jnp.sum(d_normed * x_hat, axis=0), 'sp')
        d_hat = d_normed * gain
        d_x_norm = inv_rms * (d_hat - x_hat * jnp.mean(d_hat * x_hat, axis=-1, keepdims=True))
        d_x = (dy_local.astype(F32) + d_x_norm).astype(BF16)
        unflat = lambda g, heads: jnp.transpose(g.reshape(heads, dim, d_model), (2, 0, 1))
        return y_out[None], d_x[None], unflat(d_wq, num_q), unflat(d_wk, num_kv), unflat(d_wv, num_kv), d_wo.reshape(num_q, dim, d_model), d_gain

    specs_in = (P('dp', 'sp', None), P('dp', 'sp', None), P(None), P(None, None, None), P(None, None, None), P(None, None, None), P(None, None, None))
    specs_out = (P('dp', 'sp', None), P('dp', 'sp', None), P('dp', None, None), P('dp', None, None), P('dp', None, None), P('dp', None, None), P('dp'))
    return jax.shard_map(local_step, mesh=mesh, in_specs=specs_in, out_specs=specs_out, check_vma=False)
```

time: 1320 us -> 391 us (0.30); the launches traced: 1300 us -> 387 us
  waiting for transfers between devices: 404 us -> 1.34 us
  matrix products: 457 us -> 124 us
  other arithmetic: 241 us -> 9.54 us
  Pallas kernels: 0 us -> 212 us
  local copies, waits for them, and re-layouts: 125 us -> 12.8 us
  starting transfers between devices: 40.3 us -> 0.36 us
    psum x1 -> x0, waiting for transfers between devices: 377 us -> none  [local_step(): lax.psum((d_wq, d_wk, d_wv, d_wo, d_gain), 'sp')]
    dot_general x27 -> x9, matrix products: 427 us -> 124 us  [the longest x5 100 us: dot(): return jnp.dot(a, b, preferred_element_type=F32)]
    pallas_call x0 -> x3, Pallas kernels: none -> 212 us  [the longest x1 90.6 us: attention_backward(): pl.pallas_call(functools.partial(backward_kernel, seq_par, group, scale),...]
    another operation x5 -> x0, other arithmetic: 98.5 us -> none
    reduce_sum x3 -> x0, other arithmetic: 68.2 us -> none  [one_block(): row_sum = jnp.sum(exp_scores, axis=-1, keepdims=True)]
    unnamed x81 -> x38, local copies, waits for them, and re-layouts: 67.8 us -> 6.1 us
    all_to_all x8 -> x0, starting transfers between devices: 40.3 us -> none  [the longest x1 6.01 us: local_step(): v_heads = lax.all_to_all(v_send, 'sp', 2, 1, tiled=True)]
    unnamed x5 -> x0, other arithmetic: 36.8 us -> none
  transfers between devices with their start and end apart: 9 -> 3, of which waited for: 4 -> 0; matrix products, arithmetic and copies ran while one was open for 11% -> 23% of each run, Pallas kernels for 0% -> 0%
where the time goes in v1:
time: 391 us; the launch traced here: 387 us
  Pallas kernels  212 us (54%)
  matrix products  124 us (32%)
  between operations  14.2 us (4%)
  local copies, waits for them, and re-layouts  12.8 us (3%)
  blocking collectives  12.8 us (3%)
  other arithmetic  9.54 us (2%)
    dot_general x5, matrix products, dot(): return jnp.dot(a, b, preferred_element_type=F32)  100 us
    pallas_call x1, Pallas kernels, attention_backward(): pl.pallas_call(functools.partial(backward_kernel, seq_par, group, scale),...  90.6 us
    pallas_call x1, Pallas kernels, gather_project(): pl.pallas_call(functools.partial(project_kernel, seq_par, group), in_spec...  63.5 us
    pallas_call x1, Pallas kernels, attention_forward(): pl.pallas_call(functools.partial(forward_kernel, seq_par, group, scale),...  58.1 us
    dot_general x4, matrix products, local_step(): back = lambda a, w: lax.dot_general(a, w, TN, preferred_element_type=F32)  23.8 us
    psum x1, blocking collectives, local_step(): d_gain = lax.psum(jnp.sum(d_normed * x_hat, axis=0), 'sp')  12.8 us
  transfers between devices with their start and end apart: 3, of which 0 were waited for; matrix products, arithmetic and copies ran while one was open for 23% of the time, Pallas kernels for 0%

profile of v1, /device:TPU:81, one launch (start us, length us, event | category | flops | bytes accessed | tf_op | source)
XLA Modules:
  0.0 387.0 jit_solution(9790891030125492991)
XLA Ops:
  7.3 1.9 fusion.14
  9.2 1.5 fusion.27
  10.7 1.2 fusion.11.own_ref
  11.9 1.1 constant_dynamic-slice_fusion.1
  12.9 2.8 constant_dynamic-slice_fusion
  15.7 1.3 pad_maximum_fusion.w_ref
  17.0 63.5 %gather_project.1 = (bf16[3072,2048]{1,0:T(8,128)(2,1)}, bf16[256,3072]{1,0:T(8,128)(2,1)S(1)}, bf16[64,3072]{1,0:T(8,128)(2,1)S(1)}, bf16[64,3072]{1,0:T(8,128)(2,1)S(1)}) custom-call(bf16[384,2048]{1,0:T(8,128)(2,1)S(1)} %fusion.11.own_ref, bf16[384,2048]{1,0:T(8,128)(2,1)} %pad_maximum_fusion.w_ref, f32[32,3072]{1,0:T(8,128)S(1)} %get-tuple-element.38.cos_ref, ...), custom_call_target="tpu_custom_call" | custom-call | flops 4831838208 | bytes 25165824 | tf_op jit(solution)/shard_map/gather_project/pallas_call | solution.py:225
  81.3 1.1 copy-done.7
  82.9 2.4 copy.15
  86.3 1.4 copy-done.8
  87.7 58.1 %attn_fwd.1 = (bf16[256,3072]{1,0:T(8,128)(2,1)S(1)}, f32[4,3072]{1,0:T(4,128)S(1)}, bf16[3072,2048]{1,0:T(8,128)(2,1)}) custom-call(bf16[256,3072]{1,0:T(8,128)(2,1)S(1)} %copy-done.8, bf16[3072,64]{1,0:T(8,128)(2,1)S(1)} %bitcast.49, bf16[64,3072]{1,0:T(8,128)(2,1)S(1)} %copy-done.6, bf16[384,2048]{1,0:T(8,128)(2,1)S(1)} %bitcast.48), custom_call_target="tpu_custom_call" | custom-call | flops 20937965568 | bytes 6291456 | tf_op jit(solution)/shard_map/attn_fwd/pallas_call | solution.py:311
  145.8 1.1 copy-done.9
  147.6 90.6 %attn_bwd.1 = (bf16[256,1536]{1,0:T(8,128)(2,1)}, bf16[64,3072]{1,0:T(8,128)(2,1)}, bf16[64,3072]{1,0:T(8,128)(2,1)}, bf16[2048,3072]{1,0:T(8,128)(2,1)}, bf16[2048,1536]{1,0:T(8,128)(2,1)}) custom-call(bf16[256,3072]{1,0:T(8,128)(2,1)} %copy-done.7, bf16[3072,2048]{1,0:T(8,128)(2,1)} %get-tuple-element.24.dy_ref, ...), custom_call_target="tpu_custom_call" | custom-call | flops 52344913920 | bytes 9437184 | tf_op jit(solution)/shard_map/attn_bwd/pallas_call | solution.py:439
  239.9 8.5 %fusion.16 = bf16[1,384,2048]{2,1,0:T(8,128)(2,1)} fusion(bf16[2048,2048]{1,0:T(8,128)(2,1)} %bitcast.57, bf16[1,384,2048]{2,1,0:T(8,128)(2,1)S(1)} %copy-done.12, bf16[2048,3072]{1,0:T(8,128)(2,1)} %get-tuple-element.27, s32[]{:T(128)S(6)} %select_n.37), kind=kOutput, calls=%fused_computation.22 | convolution fusion | flops 3223584768 | bytes 13107204 | tf_op jit(solution)/shard_map/dot_general | solution.py:494
  248.4 19.5 %fusion.1 = f32[2048,2048]{1,0:T(8,128)} fusion(bf16[2048,1536]{1,0:T(8,128)(2,1)} %get-tuple-element.28, bf16[3072,2048]{1,0:T(8,128)(2,1)} %get-tuple-element.32), kind=kOutput, calls=%fused_computation.2 | convolution fusion | flops 12884901888 | bytes 29360128 | tf_op jit(solution)/shard_map/dot_general | solution.py:50
  267.9 34.4 %fusion.35 = f32[2048,2048]{1,0:T(8,128)} fusion(bf16[2048,3072]{1,0:T(8,128)(2,1)} %get-tuple-element.27, bf16[3072,2048]{1,0:T(8,128)(2,1)} %get-tuple-element.24.dy_ref), kind=kOutput, calls=%fused_computation.50 | convolution fusion | flops 25769803776 | bytes 41943040 | tf_op jit(solution)/shard_map/dot_general | solution.py:50
  302.3 4.5 %fusion.25 = f32[384,2048]{1,0:T(8,128)} fusion(bf16[512,2048]{1,0:T(8,128)(2,1)} %bitcast.52, bf16[512,3072]{1,0:T(8,128)(2,1)} %all-gather.6.cloned.1.call-done, s32[]{:T(128)S(6)} %select_n.37), kind=kOutput, calls=%fused_computation.32 | convolution fusion | flops 805306368 | bytes 5636100 | tf_op jit(solution)/shard_map/dot_general | solution.py:494
  306.9 11.0 %fusion.33 = f32[512,2048]{1,0:T(8,128)} fusion(bf16[512,3072]{1,0:T(8,128)(2,1)S(1)} %copy-done.16, bf16[3072,2048]{1,0:T(8,128)(2,1)} %get-tuple-element.32), kind=kOutput, calls=%fused_computation.48 | convolution fusion | flops 6442450944 | bytes 19922944 | tf_op jit(solution)/shard_map/dot_general | solution.py:50
  317.9 12.1 %fusion.34 = f32[512,2048]{1,0:T(8,128)} fusion(bf16[512,3072]{1,0:T(8,128)(2,1)} %all-gather.8.cloned.1.call-done, bf16[3072,2048]{1,0:T(8,128)(2,1)} %get-tuple-element.32), kind=kOutput, calls=%fused_computation.49 | convolution fusion | flops 6442450944 | bytes 19922944 | tf_op jit(solution)/shard_map/dot_general | solution.py:50
  330.0 7.0 %fusion.18 = f32[384,2048]{1,0:T(8,128)S(1)} fusion(bf16[2048,2048]{1,0:T(8,128)(2,1)} %bitcast.59, bf16[2048,1536]{1,0:T(8,128)(2,1)} %all-gather.4.cloned.1.call-done, s32[]{:T(128)S(6)} %select_n.42, bf16[2048,1536]{1,0:T(8,128)(2,1)} %get-tuple-element.28, s32[]{:T(128)S(6)} %select_n.40, pred[]{:T(512)S(6)} %lt.25), kind=kOutput, calls=%fused_computation.25 | convolution fusion | flops 3222011904 | bytes 14680073 | tf_op jit(solution)/shard_map/dot_general | solution.py:494
  337.0 3.8 fusion.13
  340.8 12.8 %psum.7 = f32[2048]{0:T(1024)} all-reduce(f32[2048]{0:T(1024)S(1)} %get-tuple-element.35), channel_id=1, replica_groups=mesh['dp'=4,'sp'=8] {'sp'}, use_global_device_ids=true, to_apply=%region_3.4 | all-reduce | flops 2048 | bytes 16384 | tf_op jit(solution)/shard_map/psum | solution.py:505
  353.6 3.7 fusion.17
  357.3 23.0 %convolution_add_fusion = f32[2048,2048]{1,0:T(8,128)} fusion(f32[2048,2048]{1,0:T(8,128)} %fusion.1, bf16[2048,1536]{1,0:T(8,128)(2,1)} %all-gather.4.cloned.1.call-done, bf16[3072,2048]{1,0:T(8,128)(2,1)} %get-tuple-element.32), kind=kOutput, calls=%fused_computation | convolution fusion | flops 12889096192 | bytes 46137344 | tf_op jit(solution)/shard_map/dot_general | solution.py:50
  (48 shorter events, 4.5 us)
Async XLA Ops:
  7.2 3.5 copy-start.11
  7.2 295.2 %all-gather.6.cloned.1.call-start = ((), (), s32[]{:S(2)}) async-start(), calls=%async_computation.1 | async-start | bytes 3538944 | tf_op jit(solution)/shard_map/all_gather | solution.py:478
  9.2 2.7 copy-start.17
  10.7 6.4 %copy-start.2 = (f32[32,3072]{1,0:T(8,128)}, f32[32,3072]{1,0:T(8,128)S(1)}, u32[]{:S(2)}) copy-start(f32[32,3072]{1,0:T(8,128)S(1)} %get-tuple-element.37.sin_ref) | copy-start | bytes 1179652
  10.7 6.4 %copy-start.3 = (f32[32,3072]{1,0:T(8,128)}, f32[32,3072]{1,0:T(8,128)S(1)}, u32[]{:S(2)}) copy-start(f32[32,3072]{1,0:T(8,128)S(1)} %get-tuple-element.38.cos_ref) | copy-start | bytes 1179652
  17.0 68.3 %copy-start = (bf16[1,384,2048]{2,1,0:T(8,128)(2,1)S(1)}, bf16[1,384,2048]{2,1,0:T(8,128)(2,1)}, u32[]{:S(2)}) copy-start(bf16[1,384,2048]{2,1,0:T(8,128)(2,1)} %param.8) | copy-start | bytes 4718596
  80.6 0.7 copy-start.5
  81.3 1.1 copy-start.7
  82.5 63.4 %copy-start.4 = (bf16[64,3072]{1,0:T(8,128)(2,1)}, bf16[64,3072]{1,0:T(8,128)(2,1)S(1)}, u32[]{:S(2)}) copy-start(bf16[64,3072]{1,0:T(8,128)(2,1)S(1)} %get-tuple-element.22.kt_ref) | copy-start | bytes 1179652
  82.8 63.0 %copy-start.1 = (bf16[64,3072]{0,1:T(8,128)(2,1)}, bf16[64,3072]{0,1:T(8,128)(2,1)S(1)}, u32[]{:S(2)}) copy-start(bf16[64,3072]{0,1:T(8,128)(2,1)S(1)} %copy.14) | copy-start | bytes 1179652
  85.3 1.0 copy-start.6
  86.3 1.4 copy-start.8
  145.8 1.1 copy-start.9
  147.0 0.6 copy-start.10
  147.6 92.3 %copy-start.12 = (bf16[1,384,2048]{2,1,0:T(8,128)(2,1)S(1)}, bf16[1,384,2048]{2,1,0:T(8,128)(2,1)}, u32[]{:S(2)}) copy-start(bf16[1,384,2048]{2,1,0:T(8,128)(2,1)} %param.7) | copy-start | bytes 4718596
  238.3 79.6 %all-gather.8.cloned.1.call-start = ((), (), s32[]{:S(2)}) async-start(), calls=%async_computation.2 | async-start | bytes 3538944 | tf_op jit(solution)/shard_map/all_gather | solution.py:478
  239.1 90.9 %all-gather.4.cloned.1.call-start = ((), (), s32[]{:S(2)}) async-start(), calls=%async_computation | async-start | bytes 7077888 | tf_op jit(solution)/shard_map/all_gather | solution.py:478
  302.3 4.5 %copy-start.16 = (bf16[512,3072]{1,0:T(8,128)(2,1)S(1)}, bf16[512,3072]{1,0:T(8,128)(2,1)}, u32[]{:S(2)}) copy-start(bf16[512,3072]{1,0:T(8,128)(2,1)} %all-gather.6.cloned.1.call-done) | copy-start | bytes 9437188
  329.9 7.0 %copy-start.15 = (f32[2048]{0:T(1024)S(1)}, f32[2048]{0:T(1024)}, u32[]{:S(2)}) copy-start(f32[2048]{0:T(1024)} %param.9) | copy-start | bytes 24580
  329.9 7.0 %copy-start.18 = (f32[384]{0:T(512)S(1)}, f32[384]{0:T(512)}, u32[]{:S(2)}) copy-start(f32[384]{0:T(512)} %copy-done.17) | copy-start | bytes 4612
  330.0 7.0 %copy-start.13 = (f32[384,2048]{1,0:T(8,128)S(1)}, f32[384,2048]{1,0:T(8,128)}, u32[]{:S(2)}) copy-start(f32[384,2048]{1,0:T(8,128)} %fusion.25) | copy-start | bytes 9437188
  330.0 7.0 %copy-start.14 = (bf16[2048,8,64]{0,2,1:T(8,128)(2,1)S(1)}, bf16[2048,8,64]{0,2,1:T(8,128)(2,1)}, u32[]{:S(2)}) copy-start(bf16[2048,8,64]{0,2,1:T(8,128)(2,1)} %param.12) | copy-start | bytes 6291460
Sparse Core Ops, SparseCore 0:
  238.4 25.8 all-gather.5
  265.9 24.4 all-gather.7
  292.0 37.5 all-gather.3

commit v2 on v1

--- a/solution.py
+++ b/solution.py
@@ -42,8 +42,7 @@
 def norm_forward(x_local, gain):
     x_f32 = x_local.astype(F32)
     inv_rms = lax.rsqrt(jnp.mean(x_f32 * x_f32, axis=-1, keepdims=True) + NORM_EPS)
-    x_hat = x_f32 * inv_rms
-    return x_hat, inv_rms, (x_hat * gain).astype(BF16)
+    return (x_f32 * inv_rms * gain).astype(BF16)
 
 
 def dot(a, b):
@@ -164,9 +163,20 @@
     return pl.when(pl.program_id(0) == step)
 
 
-def project_kernel(seq_par, group, own_ref, w_ref, cos_ref, sin_ref, all_ref, q_ref, k_ref, v_ref, tile, bounce, tile_sem, bounce_sem, send_sem, recv_sem):
+def project_kernel(seq_par, group, own_ref, wq_ref, wk_ref, wv_ref, cos_ref, sin_ref, all_ref, q_ref, k_ref, v_ref, k_rows_ref, v_rows_ref, tile, bounce, w_ref, tile_sem, bounce_sem, w_sem, send_sem, recv_sem):
     rows = own_ref.shape[0]
     dim = k_ref.shape[0]
+    wide = group * dim
+    me = lax.axis_index('sp')
+    fetch = pltpu.make_async_copy(own_ref, bounce, bounce_sem)
+    fetch.start()
+    weights = [
+        pltpu.make_async_copy(wq_ref.at[pl.ds(pl.multiple_of(me * wide, wide), wide), :], w_ref.at[:wide, :], w_sem.at[0]),
+        pltpu.make_async_copy(wk_ref.at[pl.ds(pl.multiple_of(me * dim, dim), dim), :], w_ref.at[wide:wide + dim, :], w_sem.at[1]),
+        pltpu.make_async_copy(wv_ref.at[pl.ds(pl.multiple_of(me * dim, dim), dim), :], w_ref.at[wide + dim:, :], w_sem.at[2]),
+    ]
+    for copy in weights:
+        copy.start()
     greet(seq_par)
     block_of = row_place(all_ref, rows)
     ring = RingGather(seq_par, row_own(own_ref, rows), block_of, send_sem, recv_sem)
@@ -182,9 +192,12 @@
             if h < group:
                 q_ref[h * dim:(h + 1) * dim, cols] = rotate(part, cos_t, sin_t).astype(BF16)
             elif h == group:
-                k_ref[:, cols] = rotate(part, cos_t, sin_t).astype(BF16)
+                keys = rotate(part, cos_t, sin_t)
+                k_ref[:, cols] = keys.astype(BF16)
+                k_rows_ref[cols, :] = keys.T.astype(BF16)
             else:
                 v_ref[:, cols] = part.astype(BF16)
+                v_rows_ref[cols, :] = part.T.astype(BF16)
 
     def gathered(block):
         copy = pltpu.make_async_copy(block_of(block, slice(None)), tile, tile_sem)
@@ -192,8 +205,8 @@
         copy.wait()
         project(tile, block)
 
-    fetch = pltpu.make_async_copy(own_ref, bounce, bounce_sem)
-    fetch.start()
+    for copy in weights:
+        copy.wait()
     fetch.wait()
     keep = pltpu.make_async_copy(bounce, block_of(ring.me, slice(None)), bounce_sem)
     keep.start()
@@ -216,27 +229,29 @@
     ring.finish_sends()
 
 
-def gather_project(normed, w_own, cos_t, sin_t, group, seq_par):
+def gather_project(normed, wq_t, wk_t, wv_t, cos_t, sin_t, group, seq_par):
     rows, d_model = normed.shape
-    dim = w_own.shape[0] // (group + 2)
+    dim = 2 * cos_t.shape[0]
     seq = rows * seq_par
     vmem = pl.BlockSpec(memory_space=pltpu.VMEM)
     hbm = pl.BlockSpec(memory_space=pl.ANY)
     return pl.pallas_call(
         functools.partial(project_kernel, seq_par, group),
-        in_specs=[hbm, vmem, vmem, vmem],
-        out_specs=[hbm, vmem, vmem, vmem],
+        in_specs=[hbm, hbm, hbm, hbm, vmem, vmem],
+        out_specs=[hbm, vmem, vmem, vmem, vmem, vmem],
         out_shape=[
             jax.ShapeDtypeStruct((seq, d_model), BF16),
             jax.ShapeDtypeStruct((group * dim, seq), BF16),
             jax.ShapeDtypeStruct((dim, seq), BF16),
             jax.ShapeDtypeStruct((dim, seq), BF16),
+            jax.ShapeDtypeStruct((seq, dim), BF16),
+            jax.ShapeDtypeStruct((seq, dim), BF16),
         ],
-        scratch_shapes=[pltpu.VMEM((rows, d_model), BF16), pltpu.VMEM((rows, d_model), BF16), pltpu.SemaphoreType.DMA, pltpu.SemaphoreType.DMA] + GATHER_SEMS,
+        scratch_shapes=[pltpu.VMEM((rows, d_model), BF16), pltpu.VMEM((rows, d_model), BF16), pltpu.VMEM(((group + 2) * dim, d_model), BF16), pltpu.SemaphoreType.DMA, pltpu.SemaphoreType.DMA, pltpu.SemaphoreType.DMA((3,))] + GATHER_SEMS,
         compiler_params=pltpu.CompilerParams(collective_id=1, has_side_effects=True, vmem_limit_bytes=48 << 20),
         cost_estimate=pl.CostEstimate(flops=2 * seq * d_model * (group + 2) * dim, transcendentals=0, bytes_accessed=4 * seq * d_model),
         name='gather_project',
-    )(normed, w_own, cos_t, sin_t)
+    )(normed, wq_t, wk_t, wv_t, cos_t, sin_t)
 
 
 def forward_kernel(seq_par, group, scale, q_ref, k_ref, v_ref, own_ref, o_ref, lse_ref, all_ref, bounce, bounce_sem, send_sem, recv_sem):
@@ -334,7 +349,7 @@
     )(q_t, k_rows, v_t, d_out)
 
 
-def backward_kernel(seq_par, group, scale, q_ref, dy_ref, wo_ref, o_ref, lse_ref, k_ref, v_ref, kt_ref, cos_ref, sin_ref, own_ref, dqb_ref, dk_ref, dv_ref, all_ref, dqa_ref, dk_acc, dv_acc, dq_buf, bounce, bounce_sem, send_sem, recv_sem, dqa_sem, dq_send, dq_recv):
+def backward_kernel(seq_par, group, scale, q_ref, dy_ref, wo_ref, o_ref, lse_ref, k_ref, v_ref, kt_ref, cos_ref, sin_ref, own_ref, x_ref, dqb_ref, dkv_ref, y_ref, all_ref, dqa_ref, dk_acc, dv_acc, dq_buf, bounce, wo_buf, wo_sem, o_mine, o_rows, o_sem, bounce_sem, send_sem, recv_sem, dqa_sem, dq_send, dq_recv):
     block = pl.program_id(0)
     blocks = k_ref.shape[0] // BQ
     dim = k_ref.shape[1]
@@ -350,9 +365,12 @@
 
     @at_step(0)
     def _():
+        weights = pltpu.make_async_copy(wo_ref, wo_buf, wo_sem)
+        weights.start()
         greet(seq_par)
         ring.start()
         local.fetch.start()
+        weights.wait()
         dk_acc[...] = jnp.zeros_like(dk_acc)
         dv_acc[...] = jnp.zeros_like(dv_acc)
 
@@ -367,20 +385,20 @@
     @at_step(blocks * 8 // 12)
     def _():
         ring.relay_near()
-
-    @at_step(blocks * 10 // 12)
-    def _():
-        ring.relay_far()
         store = pltpu.make_async_copy(dq_buf.at[:, :half], dq_place(ring.me, slice(None)), dqa_sem)
         store.start()
         store.wait()
         dq_ring.start()
 
+    @at_step(blocks * 10 // 12)
+    def _():
+        ring.relay_far()
+
     @at_step(blocks * 11 // 12)
     def _():
         dq_ring.forward()
 
-    do_t = dot_nt(wo_ref[...], dy_ref[...]).astype(BF16)
+    do_t = dot_nt(wo_buf[pl.ds(pl.multiple_of(ring.me * rows, rows), rows), :], dy_ref[...]).astype(BF16)
     q_cat = heads_cat(q_ref, group)
     do_cat = jnp.concatenate([do_t[h * dim:(h + 1) * dim, :] for h in range(group)], axis=1)
     o_cat = heads_cat(o_ref, group)
@@ -415,21 +433,31 @@
         store = pltpu.make_async_copy(dq_buf.at[:, half:], dqb_ref, dqa_sem)
         store.start()
         dk = (dk_acc[...] * scale).astype(BF16).astype(F32)
-        dk_ref[...] = rotate_back(dk, cos_ref[...], sin_ref[...]).astype(BF16)
-        dv_ref[...] = dv_acc[...].astype(BF16)
+        dkv_ref[:dim, :] = rotate_back(dk, cos_ref[...], sin_ref[...]).astype(BF16)
+        dkv_ref[dim:, :] = dv_acc[...].astype(BF16)
         dq_ring.relay_near()
         ring.finish_recvs()
         ring.finish_sends()
         local.keep.wait()
         store.wait()
+        tokens = x_ref.shape[0]
+        fetch = pltpu.make_async_copy(all_ref.at[:, pl.ds(pl.multiple_of(ring.me * tokens, tokens), tokens)], o_mine, o_sem)
+        fetch.start()
+        fetch.wait()
+        o_rows[...] = o_mine[...].T
+        d_model = x_ref.shape[1]
+        wide_y = math.gcd(d_model, 512)
+        for start_y in range(0, d_model, wide_y):
+            cols_y = slice(start_y, start_y + wide_y)
+            y_ref[:, cols_y] = (x_ref[:, cols_y].astype(F32) + dot(o_rows[...], wo_buf[:, cols_y])).astype(BF16)
         dq_ring.relay_far()
         dq_ring.finish_recvs()
         dq_ring.finish_sends()
 
 
-def attention_backward(q_t, dy_all, wo_own, o_t, lse, k_rows, v_rows, k_t, cos_t, sin_t, group, seq_par):
+def attention_backward(x_local, q_t, dy_all, wo_t, o_t, lse, k_rows, v_rows, k_t, cos_t, sin_t, group, seq_par):
     dim, seq = k_t.shape
-    rows, d_model = wo_own.shape
+    rows, d_model = q_t.shape[0], wo_t.shape[1]
     scale = dim ** -0.5
     half = seq // 2
     pairs = seq * (seq + BQ) // 2 * group
@@ -439,20 +467,173 @@
     return pl.pallas_call(
         functools.partial(backward_kernel, seq_par, group, scale),
         grid=(seq // BQ,),
-        in_specs=[tile, pl.BlockSpec((BQ, d_model), lambda j: (j, 0)), whole(wo_own.shape), tile, pl.BlockSpec((group, BQ), lambda j: (0, j)), whole((seq, dim)), whole((seq, dim)), whole((dim, seq)), whole(cos_t.shape), whole(sin_t.shape), hbm],
-        out_specs=[hbm, whole((dim, seq)), whole((dim, seq)), hbm, hbm],
+        in_specs=[tile, pl.BlockSpec((BQ, d_model), lambda j: (j, 0)), hbm, tile, pl.BlockSpec((group, BQ), lambda j: (0, j)), whole((seq, dim)), whole((seq, dim)), whole((dim, seq)), whole(cos_t.shape), whole(sin_t.shape), hbm, whole(x_local.shape)],
+        out_specs=[hbm, whole((2 * dim, seq)), whole(x_local.shape), hbm, hbm],
         out_shape=[
             jax.ShapeDtypeStruct((rows, seq - half), BF16),
-            jax.ShapeDtypeStruct((dim, seq), BF16),
-            jax.ShapeDtypeStruct((dim, seq), BF16),
+            jax.ShapeDtypeStruct((2 * dim, seq), BF16),
+            jax.ShapeDtypeStruct(x_local.shape, BF16),
             jax.ShapeDtypeStruct((rows * seq_par, seq), BF16),
             jax.ShapeDtypeStruct((rows * seq_par, half), BF16),
         ],
-        scratch_shapes=[pltpu.VMEM((dim, seq), F32), pltpu.VMEM((dim, seq), F32), pltpu.VMEM((rows, seq), BF16), pltpu.VMEM((rows, seq), BF16), pltpu.SemaphoreType.DMA((2,))] + GATHER_SEMS + [pltpu.SemaphoreType.DMA] + GATHER_SEMS,
+        scratch_shapes=[pltpu.VMEM((dim, seq), F32), pltpu.VMEM((dim, seq), F32), pltpu.VMEM((rows, seq), BF16), pltpu.VMEM((rows, seq), BF16), pltpu.VMEM(wo_t.shape, BF16), pltpu.SemaphoreType.DMA, pltpu.VMEM((wo_t.shape[0], x_local.shape[0]), BF16), pltpu.VMEM((x_local.shape[0], wo_t.shape[0]), BF16), pltpu.SemaphoreType.DMA, pltpu.SemaphoreType.DMA((2,))] + GATHER_SEMS + [pltpu.SemaphoreType.DMA] + GATHER_SEMS,
         compiler_params=pltpu.CompilerParams(collective_id=3, has_side_effects=True, vmem_limit_bytes=56 << 20),
         cost_estimate=pl.CostEstimate(flops=40 * pairs * dim, transcendentals=pairs, bytes_accessed=12 * group * dim * seq),
         name='attn_bwd',
-    )(q_t, dy_all, wo_own, o_t, lse, k_rows, v_rows, k_t, cos_t, sin_t, o_t)
+    )(q_t, dy_all, wo_t, o_t, lse, k_rows, v_rows, k_t, cos_t, sin_t, o_t, x_local)
+
+
+def outer_kernel(*refs):
+    *parts, rhs_ref, out_ref = refs
+    start = 0
+    total = None
+    for part in parts:
+        depth = part.shape[1]
+        term = dot(part[...], rhs_ref[start:start + depth, :])
+        total = term if total is None else total + term
+        start += depth
+    out_ref[...] = total
+
+
+def weight_grad(parts, rhs, name):
+    rows = parts[0].shape[0]
+    depth, d_model = rhs.shape
+    tall = math.gcd(rows, 256)
+    return pl.pallas_call(
+        outer_kernel,
+        grid=(rows // tall,),
+        in_specs=[pl.BlockSpec((tall, p.shape[1]), lambda m: (m, 0)) for p in parts] + [pl.BlockSpec((depth, d_model), lambda m: (0, 0))],
+        out_specs=pl.BlockSpec((tall, d_model), lambda m: (m, 0)),
+        out_shape=jax.ShapeDtypeStruct((rows, d_model), F32),
+        compiler_params=pltpu.CompilerParams(vmem_limit_bytes=60 << 20),
+        cost_estimate=pl.CostEstimate(flops=2 * rows * depth * d_model, transcendentals=0, bytes_accessed=2 * depth * (rows + d_model) + 4 * rows * d_model),
+        name=name,
+    )(*parts, rhs)
+
+
+def pair_kernel(dim, lhs_ref, rhs_ref, dk_ref, dv_ref):
+    both = dot(lhs_ref[...], rhs_ref[...])
+    for h in range(dk_ref.shape[0] // dim):
+        dk_ref[h * dim:(h + 1) * dim, :] = both[2 * h * dim:(2 * h + 1) * dim, :]
+        dv_ref[h * dim:(h + 1) * dim, :] = both[(2 * h + 1) * dim:(2 * h + 2) * dim, :]
+
+
+def pair_grad(lhs, rhs, dim):
+    rows, depth = lhs.shape
+    d_model = rhs.shape[1]
+    tall = math.gcd(rows, 256)
+    out = pl.BlockSpec((tall // 2, d_model), lambda m: (m, 0))
+    return pl.pallas_call(
+        functools.partial(pair_kernel, dim),
+        grid=(rows // tall,),
+        in_specs=[pl.BlockSpec((tall, depth), lambda m: (m, 0)), pl.BlockSpec((depth, d_model), lambda m: (0, 0))],
+        out_specs=[out, out],
+        out_shape=[jax.ShapeDtypeStruct((rows // 2, d_model), F32)] * 2,
+        compiler_params=pltpu.CompilerParams(vmem_limit_bytes=60 << 20),
+        cost_estimate=pl.CostEstimate(flops=2 * rows * depth * d_model, transcendentals=0, bytes_accessed=2 * depth * (rows + d_model) + 4 * rows * d_model),
+        name='d_wkv',
+    )(lhs, rhs)
+
+
+def input_grad_kernel(seq_par, dqa_ref, dqb_ref, dkv_ref, wq_ref, wk_ref, wv_ref, x_ref, dy_ref, gain_ref, dx_ref, dgain_ref, dq_buf, dk_buf, dv_buf, wq_buf, wk_buf, wv_buf, acc, part, slots, act_sem, w_sem, send_sem, recv_sem):
+    me = lax.axis_index('sp')
+    tokens, d_model = x_ref.shape
+    half = dqa_ref.shape[1]
+    barrier = pltpu.get_barrier_semaphore()
+    for step in range(1, seq_par):
+        pl.semaphore_signal(barrier, inc=1, device_id={'sp': lax.rem(me + step, seq_par)}, device_id_type=pl.DeviceIdType.MESH)
+    low = me * tokens < half
+    first = pl.multiple_of(jnp.where(low, me * tokens, 0), 128)
+    second = pl.multiple_of(jnp.where(low, 0, me * tokens - half), 128)
+    cols = pl.ds(pl.multiple_of(me * tokens, tokens), tokens)
+    from_a = pltpu.make_async_copy(dqa_ref.at[:, pl.ds(first, tokens)], dq_buf, act_sem.at[0])
+    from_b = pltpu.make_async_copy(dqb_ref.at[:, pl.ds(second, tokens)], dq_buf, act_sem.at[0])
+
+    @pl.when(low)
+    def _():
+        from_a.start()
+
+    @pl.when(jnp.logical_not(low))
+    def _():
+        from_b.start()
+
+    take_k = pltpu.make_async_copy(dkv_ref.at[:, 0, :, cols], dk_buf, act_sem.at[1])
+    take_v = pltpu.make_async_copy(dkv_ref.at[:, 1, :, cols], dv_buf, act_sem.at[2])
+    take_k.start()
+    take_v.start()
+    chunk = wq_buf.shape[0] // 4
+    loads = [pltpu.make_async_copy(wq_ref.at[c * chunk:(c + 1) * chunk, :], wq_buf.at[c * chunk:(c + 1) * chunk, :], w_sem.at[c]) for c in range(4)]
+    loads += [pltpu.make_async_copy(wk_ref, wk_buf, w_sem.at[4]), pltpu.make_async_copy(wv_ref, wv_buf, w_sem.at[5])]
+    for copy in loads:
+        copy.start()
+    from_a.wait()
+    for c in range(4):
+        loads[c].wait()
+        term = dot(dq_buf[c * chunk:(c + 1) * chunk, :].T, wq_buf[c * chunk:(c + 1) * chunk, :])
+        if c == 0:
+            acc[...] = term
+        else:
+            acc[...] += term
+    take_k.wait()
+    take_v.wait()
+    loads[4].wait()
+    loads[5].wait()
+    acc[...] += dot(dk_buf[...].reshape(wk_buf.shape[0], tokens).T, wk_buf[...])
+    acc[...] += dot(dv_buf[...].reshape(wv_buf.shape[0], tokens).T, wv_buf[...])
+    d_normed = acc[...].astype(BF16).astype(F32)
+    acc[...] = d_normed
+    x_f32 = x_ref[...].astype(F32)
+    inv_rms = lax.rsqrt(jnp.mean(x_f32 * x_f32, axis=-1, keepdims=True) + NORM_EPS)
+    part[...] = jnp.sum(d_normed * (x_f32 * inv_rms), axis=0, keepdims=True)
+    dots = jnp.mean(acc[...] * gain_ref[...] * (x_ref[...].astype(F32) * inv_rms), axis=-1, keepdims=True)
+    x_hat = x_ref[...].astype(F32) * inv_rms
+    dx_ref[...] = (dy_ref[...].astype(F32) + inv_rms * (acc[...] * gain_ref[...] - x_hat * dots)).astype(BF16)
+    pl.semaphore_wait(barrier, seq_par - 1)
+    copies = []
+    for step in range(1, seq_par):
+        copies.append(pltpu.make_async_remote_copy(src_ref=part, dst_ref=slots.at[me], send_sem=send_sem.at[step], recv_sem=recv_sem.at[step], device_id={'sp': lax.rem(me + step, seq_par)}, device_id_type=pl.DeviceIdType.MESH))
+        copies[-1].start()
+    slots[me] = part[...]
+    for copy in copies:
+        copy.wait_recv()
+    total = slots[0]
+    for step in range(1, seq_par):
+        total = total + slots[step]
+    dgain_ref[...] = total
+    for copy in copies:
+        copy.wait_send()
+
+
+def input_grad(dqa_all, dqb_all, dkv_all, wq_t, wk_t, wv_t, x_local, dy_local, gain, dim, seq_par):
+    tokens, d_model = x_local.shape
+    num_kv = wk_t.shape[0] // dim
+    seq = dkv_all.shape[1]
+    vmem = pl.BlockSpec(memory_space=pltpu.VMEM)
+    hbm = pl.BlockSpec(memory_space=pl.ANY)
+    return pl.pallas_call(
+        functools.partial(input_grad_kernel, seq_par),
+        in_specs=[hbm] * 6 + [vmem] * 3,
+        out_specs=[vmem, vmem],
+        out_shape=[jax.ShapeDtypeStruct(x_local.shape, BF16), jax.ShapeDtypeStruct((1, d_model), F32)],
+        scratch_shapes=[
+            pltpu.VMEM((wq_t.shape[0], tokens), BF16),
+            pltpu.VMEM((num_kv, dim, tokens), BF16),
+            pltpu.VMEM((num_kv, dim, tokens), BF16),
+            pltpu.VMEM(wq_t.shape, BF16),
+            pltpu.VMEM(wk_t.shape, BF16),
+            pltpu.VMEM(wv_t.shape, BF16),
+            pltpu.VMEM((tokens, d_model), F32),
+            pltpu.VMEM((1, d_model), F32),
+            pltpu.VMEM((seq_par, 1, d_model), F32),
+            pltpu.SemaphoreType.DMA((3,)),
+            pltpu.SemaphoreType.DMA((6,)),
+            pltpu.SemaphoreType.DMA((seq_par,)),
+            pltpu.SemaphoreType.DMA((seq_par,)),
+        ],
+        compiler_params=pltpu.CompilerParams(collective_id=4, has_side_effects=True, vmem_limit_bytes=56 << 20),
+        cost_estimate=pl.CostEstimate(flops=2 * tokens * d_model * (wq_t.shape[0] + 2 * wk_t.shape[0]), transcendentals=0, bytes_accessed=2 * d_model * (wq_t.shape[0] + 2 * wk_t.shape[0])),
+        name='input_grad',
+    )(dqa_all, dqb_all, dkv_all.reshape(num_kv, 2, dim, seq), wq_t, wk_t, wv_t, x_local, dy_local, gain[None])
 
 
 def solution(mesh):
@@ -466,48 +647,29 @@
         if num_kv != seq_par or seq_par % 4:
             raise ValueError('unsupported mesh')
         seq = seq_loc * seq_par
-        index = lax.axis_index('sp')
         x_local = x_local[0]
         dy_local = dy_local[0]
         wq_t = jnp.transpose(w_q, (1, 2, 0)).reshape(num_q * dim, d_model)
         wk_t = jnp.transpose(w_k, (1, 2, 0)).reshape(num_kv * dim, d_model)
         wv_t = jnp.transpose(w_v, (1, 2, 0)).reshape(num_kv * dim, d_model)
         wo_t = w_o.reshape(num_q * dim, d_model)
-        own_q = lambda w: lax.dynamic_slice_in_dim(w, index * group * dim, group * dim, 0)
-        own_kv = lambda w: lax.dynamic_slice_in_dim(w, index * dim, dim, 0)
         gather = lambda a: lax.all_gather(a, 'sp', axis=0, tiled=True)
 
         cos_t, sin_t = rope_tables(jnp.arange(seq, dtype=F32), dim)
-        x_hat, inv_rms, normed = norm_forward(x_local, gain)
-        w_own = jnp.concatenate([own_q(wq_t), own_kv(wk_t), own_kv(wv_t)], axis=0)
-        normed_all, q_t, k_t, v_t = gather_project(normed, w_own, cos_t, sin_t, group, seq_par)
-        k_rows = k_t.T
-        v_rows = v_t.T
+        normed = norm_forward(x_local, gain)
+        normed_all, q_t, k_t, v_t, k_rows, v_rows = gather_project(normed, wq_t, wk_t, wv_t, cos_t, sin_t, group, seq_par)
         o_t, lse, dy_all = attention_forward(q_t, k_rows, v_t, dy_local, group, seq_par)
-        dqb_t, dk_t, dv_t, o_all, dqa_all = attention_backward(q_t, dy_all, own_q(wo_t), o_t, lse, k_rows, v_rows, k_t, cos_t, sin_t, group, seq_par)
+        dqb_t, dkv_t, y_out, o_all, dqa_all = attention_backward(x_local, q_t, dy_all, wo_t, o_t, lse, k_rows, v_rows, k_t, cos_t, sin_t, group, seq_par)
         dqb_all = gather(dqb_t)
-        dk_all = gather(dk_t)
-        dv_all = gather(dv_t)
-        half = seq // 2
-        at_col = lambda a, start: lax.dynamic_slice_in_dim(a, start, seq_loc, 1)
-        mine = lambda a: at_col(a, index * seq_loc)
-        back = lambda a, w: lax.dot_general(a, w, TN, preferred_element_type=F32)
-        low = index * seq_loc < half
-        dq_mine = jnp.where(low, at_col(dqa_all, jnp.where(low, index * seq_loc, 0)), at_col(dqb_all, jnp.where(low, 0, index * seq_loc - half)))
-        y_out = (x_local.astype(F32) + back(mine(o_all), wo_t)).astype(BF16)
-        d_wo = dot(o_all, dy_all)
-        d_wqa = dot(dqa_all, normed_all[:half])
-        d_wqa, dqb_all = lax.optimization_barrier((d_wqa, dqb_all))
-        d_wq = d_wqa + dot(dqb_all, normed_all[half:])
-        d_wk = dot(dk_all, normed_all)
-        d_wv = dot(dv_all, normed_all)
-        d_normed = (back(dq_mine, wq_t) + back(mine(dk_all), wk_t) + back(mine(dv_all), wv_t)).astype(BF16).astype(F32)
-        d_gain = lax.psum(jnp.sum(d_normed * x_hat, axis=0), 'sp')
-        d_hat = d_normed * gain
-        d_x_norm = inv_rms * (d_hat - x_hat * jnp.mean(d_hat * x_hat, axis=-1, keepdims=True))
-        d_x = (dy_local.astype(F32) + d_x_norm).astype(BF16)
+        d_wo = weight_grad([o_all], dy_all, 'd_wo')
+        dkv_t, d_wo = lax.optimization_barrier((dkv_t, d_wo))
+        dkv_all = gather(dkv_t)
+        d_wq = weight_grad([dqa_all, dqb_all], normed_all, 'd_wq')
+        dkv_all, d_wq = lax.optimization_barrier((dkv_all, d_wq))
+        d_wk, d_wv = pair_grad(dkv_all, normed_all, dim)
+        d_x, d_gain = input_grad(dqa_all, dqb_all, dkv_all, wq_t, wk_t, wv_t, x_local, dy_local, gain, dim, seq_par)
         unflat = lambda g, heads: jnp.transpose(g.reshape(heads, dim, d_model), (2, 0, 1))
-        return y_out[None], d_x[None], unflat(d_wq, num_q), unflat(d_wk, num_kv), unflat(d_wv, num_kv), d_wo.reshape(num_q, dim, d_model), d_gain
+        return y_out[None], d_x[None], unflat(d_wq, num_q), unflat(d_wk, num_kv), unflat(d_wv, num_kv), d_wo.reshape(num_q, dim, d_model), d_gain[0]
 
     specs_in = (P('dp', 'sp', None), P('dp', 'sp', None), P(None), P(None, None, None), P(None, None, None), P(None, None, None), P(None, None, None))
     specs_out = (P('dp', 'sp', None), P('dp', 'sp', None), P('dp', None, None), P('dp', None, None), P('dp', None, None), P('dp', None, None), P('dp'))

time: 391 us -> 351 us (0.90)
  matrix products: 124 us -> 0 us
  Pallas kernels: 212 us -> 314 us
  blocking collectives: 12.8 us -> 0 us
  waiting for transfers between devices: 1.34 us -> 11.4 us
  local copies, waits for them, and re-layouts: 12.8 us -> 5.49 us
    dot_general x9 -> x0, matrix products: 124 us -> none  [the longest x5 100 us: dot(): return jnp.dot(a, b, preferred_element_type=F32)]
    pallas_call x0 -> x4, Pallas kernels: none -> 105 us  [the longest x2 67.8 us: weight_grad(): pl.pallas_call(outer_kernel, grid=(rows // tall,), in_specs=[pl.BlockSpec...]
    psum x1 -> x0, blocking collectives: 12.8 us -> none  [local_step(): d_gain = lax.psum(jnp.sum(d_normed * x_hat, axis=0), 'sp')]
    all_gather x3 -> x2, waiting for transfers between devices: 0.01 us -> 11.3 us  [local_step(): gather = lambda a: lax.all_gather(a, 'sp', axis=0, tiled=True)]
  transfers between devices with their start and end apart: 3 -> 2, of which waited for: 0 -> 2; matrix products, arithmetic and copies ran while one was open for 23% -> 0% of each run, Pallas kernels for 0% -> 19%
where the time goes in v2:
time: 351 us
  Pallas kernels  314 us (89%)
  between operations  14.3 us (4%)
  waiting for transfers between devices  11.4 us (3%)
  other arithmetic  5.68 us (2%)
  local copies, waits for them, and re-layouts  5.49 us (2%)
    pallas_call x1, Pallas kernels, attention_backward(): pl.pallas_call(functools.partial(backward_kernel, seq_par, group, scale),...  89 us
    pallas_call x2, Pallas kernels, weight_grad(): pl.pallas_call(outer_kernel, grid=(rows // tall,), in_specs=[pl.BlockSpec...  67.8 us
    pallas_call x1, Pallas kernels, gather_project(): pl.pallas_call(functools.partial(project_kernel, seq_par, group), in_spec...  62.1 us
    pallas_call x1, Pallas kernels, attention_forward(): pl.pallas_call(functools.partial(forward_kernel, seq_par, group, scale),...  58.3 us
    pallas_call x1, Pallas kernels, pair_grad(): pl.pallas_call(functools.partial(pair_kernel, dim), grid=(rows // tall,),...  20 us
    pallas_call x1, Pallas kernels, input_grad(): pl.pallas_call(functools.partial(input_grad_kernel, seq_par), in_specs=[h...  16.7 us
    all_gather x2, waiting for transfers between devices, local_step(): gather = lambda a: lax.all_gather(a, 'sp', axis=0, tiled=True)  11.3 us
  transfers between devices with their start and end apart: 2, of which 2 were waited for; matrix products, arithmetic and copies ran while one was open for 0% of the time, Pallas kernels for 19%

profile of v2, /device:TPU:81, one launch (start us, length us, event | category | flops | bytes accessed | tf_op | source)
XLA Modules:
  0.0 350.9 jit_solution(16395575673155819306)
XLA Ops:
  7.2 0.0 copy-start.9
  7.2 0.1 all-gather.3.cloned.1.call-start
  7.3 1.9 fusion
  9.2 1.5 fusion.3
  10.7 2.3 fusion.2.own_ref
  13.0 62.1 %gather_project.1 = (bf16[3072,2048]{1,0:T(8,128)(2,1)}, bf16[256,3072]{1,0:T(8,128)(2,1)S(1)}, bf16[64,3072]{1,0:T(8,128)(2,1)S(1)}, bf16[64,3072]{1,0:T(8,128)...) custom-call(bf16[384,2048]{1,0:T(8,128)(2,1)} %fusion.2.own_ref, bf16[2048,2048]{1,0:T(8,128)(2,1)} %bitcast.33, ...), custom_call_target="tpu_custom_call" | custom-call | flops 4831838208 | bytes 25165824 | tf_op jit(solution)/shard_map/gather_project/pallas_call | solution.py:238
  75.2 0.0 copy-start.5
  75.2 58.3 %attn_fwd.1 = (bf16[256,3072]{1,0:T(8,128)(2,1)S(1)}, f32[4,3072]{1,0:T(4,128)S(1)}, bf16[3072,2048]{1,0:T(8,128)(2,1)}) custom-call(bf16[256,3072]{1,0:T(8,128)(2,1)S(1)} %get-tuple-element.29.q_ref, bf16[3072,64]{1,0:T(8,128)(2,1)S(1)} %get-tuple-element.30.k_ref, bf16[64,3072]{1,0:T(8,128)(2,1)S(1)} %get-tuple-element.31.v_ref, bf16[384,2048]{1,0:T(8,128)(2,1)S(1)} %bitcast.30), custom_call_target="tpu_custom_call" | custom-call | flops 20937965568 | bytes 6291456 | tf_op jit(solution)/shard_map/attn_fwd/pallas_call | solution.py:326
  133.6 1.1 copy-done.7
  134.7 0.6 copy-done.8
  135.3 89.0 %attn_bwd.1 = (bf16[256,1536]{1,0:T(8,128)(2,1)}, bf16[128,3072]{1,0:T(8,128)(2,1)}, bf16[384,2048]{1,0:T(8,128)(2,1)}, bf16[2048,3072]{1,0:T(8,128)(2,1)}, bf16[2048,1536]{1,0:T(8,128)(2,1)}) custom-call(bf16[256,3072]{1,0:T(8,128)(2,1)} %copy-done.3, bf16[3072,2048]{1,0:T(8,128)(2,1)} %get-tuple-element.32.dy_ref.refs_1_, bf16[2048,2048]{1,0:T(8,128)(2,1)} %bitcast.44, ...), custom_call_target="tpu_custom_call" | custom-call | flops 52344913920 | bytes 9437184 | tf_op jit(solution)/shard_map/attn_bwd/pallas_call | solution.py:467
  224.3 0.1 all-gather.3.cloned.1.call-update
  224.4 0.1 all-gather.5.cloned.1.call-start
  224.4 34.0 %d_wo.1 = f32[2048,2048]{1,0:T(8,128)} custom-call(bf16[2048,3072]{1,0:T(8,128)(2,1)} %get-tuple-element.41.refs_0_, bf16[3072,2048]{1,0:T(8,128)(2,1)} %get-tuple-element.32.dy_ref.refs_1_), custom_call_target="tpu_custom_call" | custom-call | flops 25769803776 | bytes 41943040 | tf_op jit(solution)/shard_map/d_wo/pallas_call | solution.py:502
  258.4 0.1 all-gather.5.cloned.1.call-update
  258.5 5.8 %all-gather.3.cloned.1.call-done.refs_1_.dqb_ref = bf16[2048,1536]{1,0:T(8,128)(2,1)} async-done(((bf16[256,1536]{1,0:T(8,128)(2,1)}), bf16[2048,1536]{1,0:T(8,128)(2,1)}) %all-gather.3.cloned.1.call-update) | async-done | bytes 6291472 | tf_op jit(solution)/shard_map/all_gather | solution.py:656
  264.3 33.8 %d_wq.1 = f32[2048,2048]{1,0:T(8,128)} custom-call(bf16[2048,1536]{1,0:T(8,128)(2,1)} %get-tuple-element.38.refs_0_.dqa_ref, bf16[2048,1536]{1,0:T(8,128)(2,1)} %all-gather.3.cloned.1.call-done.refs_1_.dqb_ref, bf16[3072,2048]{1,0:T(8,128)(2,1)} %get-tuple-element.43.refs_2_.rhs_ref), custom_call_target="tpu_custom_call" | custom-call | flops 25769803776 | bytes 41943040 | tf_op jit(solution)/shard_map/d_wq/pallas_call | solution.py:502
  298.1 5.4 %all-gather.5.cloned.1.call-done.lhs_ref = bf16[1024,3072]{1,0:T(8,128)(2,1)} async-done(((bf16[128,3072]{1,0:T(8,128)(2,1)}), bf16[1024,3072]{1,0:T(8,128)(2,1)}) %all-gather.5.cloned.1.call-update) | async-done | bytes 6291472 | tf_op jit(solution)/shard_map/all_gather | solution.py:656
  303.6 20.0 %d_wkv.1 = (f32[512,2048]{1,0:T(8,128)}, f32[512,2048]{1,0:T(8,128)}) custom-call(bf16[1024,3072]{1,0:T(8,128)(2,1)} %all-gather.5.cloned.1.call-done.lhs_ref, bf16[3072,2048]{1,0:T(8,128)(2,1)} %get-tuple-element.43.refs_2_.rhs_ref), custom_call_target="tpu_custom_call" | custom-call | flops 12884901888 | bytes 27262976 | tf_op jit(solution)/shard_map/d_wkv/pallas_call | solution.py:526
  323.6 16.7 %input_grad.1 = (bf16[384,2048]{1,0:T(8,128)(2,1)}, f32[1,2048]{1,0:T(1,128)}) custom-call(bf16[2048,1536]{1,0:T(8,128)(2,1)} %get-tuple-element.38.refs_0_.dqa_ref, bf16[2048,1536]{1,0:T(8,128)(2,1)} %all-gather.3.cloned.1.call-done.refs_1_.dqb_ref, bf16[8,2,64,3072]{3,2,1,0:T(8,128)(2,1)} %bitcast.35, bf16[2048,2048]{1,0:T(8,128)(2,1)} %bitcast.34, ...), custom_call_target="tpu_custom_call" | custom-call | flops 4831838208 | bytes 12582912 | tf_op jit(solution)/shard_map/input_grad/pallas_call | solution.py:613
  340.4 1.1 copy.17
  341.5 0.8 copy-done.11
  342.3 1.1 copy.18
  343.5 0.6 copy.19
  (23 shorter events, 0.1 us)
Async XLA Ops:
  7.2 3.5 copy-start.9
  7.2 257.1 %all-gather.3.cloned.1.call-start = ((), (), s32[]{:S(2)}) async-start(), calls=%async_computation | async-start | bytes 7077888 | tf_op jit(solution)/shard_map/all_gather | solution.py:656
  10.7 64.5 %copy-start.1 = (f32[32,3072]{1,0:T(8,128)}, f32[32,3072]{1,0:T(8,128)S(1)}, u32[]{:S(2)}) copy-start(f32[32,3072]{1,0:T(8,128)S(1)} %get-tuple-element.51.sin_ref) | copy-start | bytes 1179652
  10.7 64.5 %copy-start.2 = (f32[32,3072]{1,0:T(8,128)}, f32[32,3072]{1,0:T(8,128)S(1)}, u32[]{:S(2)}) copy-start(f32[32,3072]{1,0:T(8,128)S(1)} %get-tuple-element.52.cos_ref) | copy-start | bytes 1179652
  13.0 62.2 %copy-start = (bf16[1,384,2048]{2,1,0:T(8,128)(2,1)S(1)}, bf16[1,384,2048]{2,1,0:T(8,128)(2,1)}, u32[]{:S(2)}) copy-start(bf16[1,384,2048]{2,1,0:T(8,128)(2,1)} %param.8) | copy-start | bytes 4718596
  75.1 58.4 %copy-start.3 = (bf16[256,3072]{1,0:T(8,128)(2,1)}, bf16[256,3072]{1,0:T(8,128)(2,1)S(1)}, u32[]{:S(2)}) copy-start(bf16[256,3072]{1,0:T(8,128)(2,1)S(1)} %get-tuple-element.29.q_ref) | copy-start | bytes 4718596
  75.2 58.4 %copy-start.4 = (bf16[3072,64]{1,0:T(8,128)(2,1)}, bf16[3072,64]{1,0:T(8,128)(2,1)S(1)}, u32[]{:S(2)}) copy-start(bf16[3072,64]{1,0:T(8,128)(2,1)S(1)} %get-tuple-element.30.k_ref) | copy-start | bytes 1179652
  75.2 58.4 %copy-start.5 = (bf16[3072,64]{1,0:T(8,128)(2,1)}, bf16[3072,64]{1,0:T(8,128)(2,1)S(1)}, u32[]{:S(2)}) copy-start(bf16[3072,64]{1,0:T(8,128)(2,1)S(1)} %get-tuple-element.35.v_ref) | copy-start | bytes 1179652
  75.2 58.4 %copy-start.6 = (bf16[64,3072]{1,0:T(8,128)(2,1)}, bf16[64,3072]{1,0:T(8,128)(2,1)S(1)}, u32[]{:S(2)}) copy-start(bf16[64,3072]{1,0:T(8,128)(2,1)S(1)} %get-tuple-element.36.kt_ref) | copy-start | bytes 1179652
  133.6 1.1 copy-start.7
  134.7 0.6 copy-start.8
  224.4 79.2 %all-gather.5.cloned.1.call-start = ((), (), s32[]{:S(2)}) async-start(), calls=%async_computation.1 | async-start | bytes 7077888 | tf_op jit(solution)/shard_map/all_gather | solution.py:656
  323.6 16.8 %copy-start.10 = (bf16[384,2048]{1,0:T(8,128)(2,1)S(1)}, bf16[384,2048]{1,0:T(8,128)(2,1)}, u32[]{:S(2)}) copy-start(bf16[384,2048]{1,0:T(8,128)(2,1)} %get-tuple-element.37) | copy-start | bytes 4718596
  340.4 2.0 copy-start.11
  340.4 3.1 copy-start.12
Sparse Core Ops, SparseCore 0:
  224.5 39.7 all-gather.2
  265.9 37.6 all-gather.4

commit v3 on v2

--- a/solution.py
+++ b/solution.py
@@ -119,11 +119,13 @@
 GATHER_SEMS = [pltpu.SemaphoreType.DMA((10,)), pltpu.SemaphoreType.DMA((10,))]
 
 
-def greet(seq_par):
+def greet(seq_par, meanwhile=None):
     me = lax.axis_index('sp')
     barrier = pltpu.get_barrier_semaphore()
     for peer in (me + 1 - 2 * lax.rem(me, 2), lax.rem(me + 2, seq_par), lax.rem(me + seq_par - 2, seq_par)):
         pl.semaphore_signal(barrier, inc=1, device_id={'sp': peer}, device_id_type=pl.DeviceIdType.MESH)
+    if meanwhile is not None:
+        meanwhile()
     pl.semaphore_wait(barrier, 3)
 
 
@@ -163,27 +165,21 @@
     return pl.when(pl.program_id(0) == step)
 
 
-def project_kernel(seq_par, group, own_ref, wq_ref, wk_ref, wv_ref, cos_ref, sin_ref, all_ref, q_ref, k_ref, v_ref, k_rows_ref, v_rows_ref, tile, bounce, w_ref, tile_sem, bounce_sem, w_sem, send_sem, recv_sem):
-    rows = own_ref.shape[0]
+def forward_kernel(seq_par, group, scale, x_ref, gain_ref, wq_ref, wk_ref, wv_ref, cos_ref, sin_ref, dy_ref, all_ref, q_ref, k_ref, k_rows_ref, v_rows_ref, o_ref, lse_ref, dy_all, v_ref, tile, bounce, w_ref, dy_bounce, tile_sem, bounce_sem, w_sem, dy_sem, send_sem, recv_sem, dy_send, dy_recv):
+    block = pl.program_id(0)
+    rows = x_ref.shape[0]
     dim = k_ref.shape[0]
+    blocks = k_ref.shape[1] // BQ
     wide = group * dim
+    block_of = row_place(all_ref, rows)
+    dy_place = row_place(dy_all, rows)
     me = lax.axis_index('sp')
-    fetch = pltpu.make_async_copy(own_ref, bounce, bounce_sem)
-    fetch.start()
-    weights = [
-        pltpu.make_async_copy(wq_ref.at[pl.ds(pl.multiple_of(me * wide, wide), wide), :], w_ref.at[:wide, :], w_sem.at[0]),
-        pltpu.make_async_copy(wk_ref.at[pl.ds(pl.multiple_of(me * dim, dim), dim), :], w_ref.at[wide:wide + dim, :], w_sem.at[1]),
-        pltpu.make_async_copy(wv_ref.at[pl.ds(pl.multiple_of(me * dim, dim), dim), :], w_ref.at[wide + dim:, :], w_sem.at[2]),
-    ]
-    for copy in weights:
-        copy.start()
-    greet(seq_par)
-    block_of = row_place(all_ref, rows)
-    ring = RingGather(seq_par, row_own(own_ref, rows), block_of, send_sem, recv_sem)
-    ring.start()
-
-    def project(rows_ref, block):
-        cols = pl.ds(pl.multiple_of(block * rows, rows), rows)
+    ring = RingGather(seq_par, lambda part: block_of(me, part), block_of, send_sem, recv_sem)
+    dy_ring = RingGather(seq_par, row_own(dy_ref, rows), dy_place, dy_send, dy_recv)
+    dy_local = Bounce(dy_ref, dy_bounce, dy_place(ring.me, slice(None)), dy_sem)
+
+    def project(rows_ref, source):
+        cols = pl.ds(pl.multiple_of(source * rows, rows), rows)
         cos_t = cos_ref[:, cols]
         sin_t = sin_ref[:, cols]
         lin = dot_nt(w_ref[...], rows_ref[...])
@@ -199,99 +195,72 @@
                 v_ref[:, cols] = part.astype(BF16)
                 v_rows_ref[cols, :] = part.T.astype(BF16)
 
-    def gathered(block):
-        copy = pltpu.make_async_copy(block_of(block, slice(None)), tile, tile_sem)
+    def gathered(source):
+        copy = pltpu.make_async_copy(block_of(source, slice(None)), tile, tile_sem)
         copy.start()
         copy.wait()
-        project(tile, block)
-
-    for copy in weights:
-        copy.wait()
-    fetch.wait()
-    keep = pltpu.make_async_copy(bounce, block_of(ring.me, slice(None)), bounce_sem)
-    keep.start()
-    project(bounce, ring.me)
-    ring.p0.wait_recv()
-    gathered(ring.partner)
-    ring.forward()
-    ring.relay_near()
-    gathered(ring.left)
-    gathered(ring.right)
-    ring.p1.wait_recv()
-    gathered(ring.other(ring.left))
-    ring.p2.wait_recv()
-    gathered(ring.other(ring.right))
-    ring.relay_far()
-    gathered(ring.far)
-    ring.p3.wait_recv()
-    gathered(ring.other(ring.far))
-    keep.wait()
-    ring.finish_sends()
-
-
-def gather_project(normed, wq_t, wk_t, wv_t, cos_t, sin_t, group, seq_par):
-    rows, d_model = normed.shape
-    dim = 2 * cos_t.shape[0]
-    seq = rows * seq_par
-    vmem = pl.BlockSpec(memory_space=pltpu.VMEM)
-    hbm = pl.BlockSpec(memory_space=pl.ANY)
-    return pl.pallas_call(
-        functools.partial(project_kernel, seq_par, group),
-        in_specs=[hbm, hbm, hbm, hbm, vmem, vmem],
-        out_specs=[hbm, vmem, vmem, vmem, vmem, vmem],
-        out_shape=[
-            jax.ShapeDtypeStruct((seq, d_model), BF16),
-            jax.ShapeDtypeStruct((group * dim, seq), BF16),
-            jax.ShapeDtypeStruct((dim, seq), BF16),
-            jax.ShapeDtypeStruct((dim, seq), BF16),
-            jax.ShapeDtypeStruct((seq, dim), BF16),
-            jax.ShapeDtypeStruct((seq, dim), BF16),
-        ],
-        scratch_shapes=[pltpu.VMEM((rows, d_model), BF16), pltpu.VMEM((rows, d_model), BF16), pltpu.VMEM(((group + 2) * dim, d_model), BF16), pltpu.SemaphoreType.DMA, pltpu.SemaphoreType.DMA, pltpu.SemaphoreType.DMA((3,))] + GATHER_SEMS,
-        compiler_params=pltpu.CompilerParams(collective_id=1, has_side_effects=True, vmem_limit_bytes=48 << 20),
-        cost_estimate=pl.CostEstimate(flops=2 * seq * d_model * (group + 2) * dim, transcendentals=0, bytes_accessed=4 * seq * d_model),
-        name='gather_project',
-    )(normed, wq_t, wk_t, wv_t, cos_t, sin_t)
-
-
-def forward_kernel(seq_par, group, scale, q_ref, k_ref, v_ref, own_ref, o_ref, lse_ref, all_ref, bounce, bounce_sem, send_sem, recv_sem):
-    block = pl.program_id(0)
-    blocks = k_ref.shape[0] // BQ
-    rows = own_ref.shape[0]
-    place = row_place(all_ref, rows)
-    ring = RingGather(seq_par, row_own(own_ref, rows), place, send_sem, recv_sem)
-    local = Bounce(own_ref, bounce, place(ring.me, slice(None)), bounce_sem)
+        project(tile, source)
 
     @at_step(0)
     def _():
-        greet(seq_par)
+        weights = [
+            pltpu.make_async_copy(wq_ref.at[pl.ds(pl.multiple_of(me * wide, wide), wide), :], w_ref.at[:wide, :], w_sem.at[0]),
+            pltpu.make_async_copy(wk_ref.at[pl.ds(pl.multiple_of(me * dim, dim), dim), :], w_ref.at[wide:wide + dim, :], w_sem.at[1]),
+            pltpu.make_async_copy(wv_ref.at[pl.ds(pl.multiple_of(me * dim, dim), dim), :], w_ref.at[wide + dim:, :], w_sem.at[2]),
+        ]
+        for copy in weights:
+            copy.start()
+        keep = pltpu.make_async_copy(bounce, block_of(me, slice(None)), bounce_sem)
+
+        def norm():
+            bounce[...] = norm_forward(x_ref[...], gain_ref[...])
+            keep.start()
+            keep.wait()
+
+        greet(seq_par, norm)
         ring.start()
-        local.fetch.start()
-
-    @at_step(1)
-    def _():
-        local.turn()
-
-    @at_step(blocks * 7 // 12)
-    def _():
+        for copy in weights:
+            copy.wait()
+        project(bounce, me)
+        ring.p0.wait_recv()
+        gathered(ring.partner)
         ring.forward()
-
-    @at_step(blocks * 10 // 12)
-    def _():
+        dy_ring.start()
+        dy_local.fetch.start()
         ring.relay_near()
-
-    dim = k_ref.shape[1]
-    wide = group * BQ
-    q_cat = heads_cat(q_ref, group)
+        gathered(ring.left)
+        gathered(ring.right)
+        ring.p1.wait_recv()
+        gathered(ring.other(ring.left))
+        ring.p2.wait_recv()
+        gathered(ring.other(ring.right))
+        ring.relay_far()
+        gathered(ring.far)
+        ring.p3.wait_recv()
+        gathered(ring.other(ring.far))
+        dy_local.turn()
+        ring.finish_sends()
+
+    @at_step(blocks * 5 // 12)
+    def _():
+        dy_ring.forward()
+
+    @at_step(blocks * 9 // 12)
+    def _():
+        dy_ring.relay_near()
+
+    cols_q = pl.ds(pl.multiple_of(block * BQ, BQ), BQ)
+    q_cat = jnp.concatenate([q_ref[h * dim:(h + 1) * dim, cols_q] for h in range(group)], axis=1)
+    wide_q = group * BQ
     factor = scale * LOG2E
 
     def step(start, carry, masked):
         m_old, l_old, acc = carry
-        keys = k_ref[pl.ds(start, BK), :]
+        keys = k_rows_ref[pl.ds(start, BK), :]
         scores = dot(keys, q_cat) * factor
         if masked:
-            row = lax.broadcasted_iota(jnp.int32, (BK, wide), 0)
-            col = lax.broadcasted_iota(jnp.int32, (BK, wide), 1) % BQ
+            row = lax.broadcasted_iota(jnp.int32, (BK, wide_q), 0)
+            col = lax.broadcasted_iota(jnp.int32, (BK, wide_q), 1) % BQ
             scores = jnp.where(row <= col, scores, -1e30)
         m_new = jnp.maximum(m_old, jnp.max(scores, axis=0, keepdims=True))
         probs = jnp.exp2(scores - m_new)
@@ -300,7 +269,7 @@
         out = dot(v_ref[:, pl.ds(start, BK)], probs.astype(BF16))
         return m_new, l_new, acc * alpha + out
 
-    init = (jnp.full((1, wide), -1e30, F32), jnp.zeros((1, wide), F32), jnp.zeros((dim, wide), F32))
+    init = (jnp.full((1, wide_q), -1e30, F32), jnp.zeros((1, wide_q), F32), jnp.zeros((dim, wide_q), F32))
     carry = lax.fori_loop(0, block, lambda i, c: step(pl.multiple_of(i * BK, BK), c, False), init)
     m_fin, l_fin, acc = step(pl.multiple_of(block * BK, BK), carry, True)
     out = (acc / l_fin).astype(BF16)
@@ -311,42 +280,50 @@
 
     @at_step(blocks - 1)
     def _():
-        ring.relay_far()
-        local.keep.wait()
-        ring.finish_recvs()
-        ring.finish_sends()
-
-
-def attention_forward(q_t, k_rows, v_t, d_out, group, seq_par):
-    dim, seq = v_t.shape
-    rows, d_model = d_out.shape
+        dy_ring.relay_far()
+        dy_local.keep.wait()
+        dy_ring.finish_recvs()
+        dy_ring.finish_sends()
+
+
+def attention_forward(x_local, gain, wq_t, wk_t, wv_t, cos_t, sin_t, d_out, group, seq_par):
+    rows, d_model = x_local.shape
+    dim = 2 * cos_t.shape[0]
+    seq = rows * seq_par
     scale = dim ** -0.5
     pairs = seq * (seq + BQ) // 2 * group
     hbm = pl.BlockSpec(memory_space=pl.ANY)
+    whole = lambda shape: pl.BlockSpec(shape, lambda j: (0, 0))
+    shapes = [(group * dim, seq), (dim, seq), (seq, dim), (seq, dim)]
     return pl.pallas_call(
         functools.partial(forward_kernel, seq_par, group, scale),
         grid=(seq // BQ,),
-        in_specs=[
-            pl.BlockSpec((group * dim, BQ), lambda j: (0, j)),
-            pl.BlockSpec((seq, dim), lambda j: (0, 0)),
-            pl.BlockSpec((dim, seq), lambda j: (0, 0)),
-            hbm,
-        ],
-        out_specs=[
+        in_specs=[whole(x_local.shape), whole((1, d_model)), hbm, hbm, hbm, whole(cos_t.shape), whole(sin_t.shape), hbm],
+        out_specs=[hbm] + [whole(shape) for shape in shapes] + [
             pl.BlockSpec((group * dim, BQ), lambda j: (0, j)),
             pl.BlockSpec((group, BQ), lambda j: (0, j)),
             hbm,
         ],
-        out_shape=[
+        out_shape=[jax.ShapeDtypeStruct((seq, d_model), BF16)] + [jax.ShapeDtypeStruct(shape, BF16) for shape in shapes] + [
             jax.ShapeDtypeStruct((group * dim, seq), BF16),
             jax.ShapeDtypeStruct((group, seq), F32),
             jax.ShapeDtypeStruct((seq, d_model), BF16),
         ],
-        scratch_shapes=[pltpu.VMEM((rows, d_model), BF16), pltpu.SemaphoreType.DMA((2,))] + GATHER_SEMS,
-        compiler_params=pltpu.CompilerParams(collective_id=2, has_side_effects=True, vmem_limit_bytes=48 << 20),
-        cost_estimate=pl.CostEstimate(flops=16 * pairs * dim, transcendentals=pairs, bytes_accessed=8 * group * dim * seq),
+        scratch_shapes=[
+            pltpu.VMEM((dim, seq), BF16),
+            pltpu.VMEM((rows, d_model), BF16),
+            pltpu.VMEM((rows, d_model), BF16),
+            pltpu.VMEM(((group + 2) * dim, d_model), BF16),
+            pltpu.VMEM((rows, d_model), BF16),
+            pltpu.SemaphoreType.DMA,
+            pltpu.SemaphoreType.DMA,
+            pltpu.SemaphoreType.DMA((3,)),
+            pltpu.SemaphoreType.DMA((2,)),
+        ] + GATHER_SEMS + GATHER_SEMS,
+        compiler_params=pltpu.CompilerParams(collective_id=1, has_side_effects=True, vmem_limit_bytes=62 << 20),
+        cost_estimate=pl.CostEstimate(flops=16 * pairs * dim, transcendentals=pairs, bytes_accessed=8 * seq * d_model),
         name='attn_fwd',
-    )(q_t, k_rows, v_t, d_out)
+    )(x_local, gain[None], wq_t, wk_t, wv_t, cos_t, sin_t, d_out)
 
 
 def backward_kernel(seq_par, group, scale, q_ref, dy_ref, wo_ref, o_ref, lse_ref, k_ref, v_ref, kt_ref, cos_ref, sin_ref, own_ref, x_ref, dqb_ref, dkv_ref, y_ref, all_ref, dqa_ref, dk_acc, dv_acc, dq_buf, bounce, wo_buf, wo_sem, o_mine, o_rows, o_sem, bounce_sem, send_sem, recv_sem, dqa_sem, dq_send, dq_recv):
@@ -483,56 +460,173 @@
     )(q_t, dy_all, wo_t, o_t, lse, k_rows, v_rows, k_t, cos_t, sin_t, o_t, x_local)
 
 
-def outer_kernel(*refs):
-    *parts, rhs_ref, out_ref = refs
-    start = 0
-    total = None
-    for part in parts:
-        depth = part.shape[1]
-        term = dot(part[...], rhs_ref[start:start + depth, :])
-        total = term if total is None else total + term
-        start += depth
-    out_ref[...] = total
-
-
-def weight_grad(parts, rhs, name):
-    rows = parts[0].shape[0]
-    depth, d_model = rhs.shape
-    tall = math.gcd(rows, 256)
+def tail_gather_kernel(seq_par, dim, o_ref, dy_ref, r_ref, dqb_own, dkv_own, dwo_ref, dk_ref, dv_ref, dqb_ref, dkv_ref, dy_buf, r_buf, dkv_buf, load_sem, dkv_sem, dqb_bounce, dkv_bounce, dqb_local, dkv_local, dqb_send, dqb_recv, dkv_send, dkv_recv):
+    tile = pl.program_id(0)
+    short = dkv_buf.shape[1]
+    dqb_place = row_place(dqb_ref, dqb_own.shape[0])
+    dkv_place = row_place(dkv_ref, dkv_own.shape[0])
+    dqb = RingGather(seq_par, row_own(dqb_own, dqb_own.shape[0]), dqb_place, dqb_send, dqb_recv)
+    dkv = RingGather(seq_par, row_own(dkv_own, dkv_own.shape[0]), dkv_place, dkv_send, dkv_recv)
+    keep_dqb = Bounce(dqb_own, dqb_bounce, dqb_place(dqb.me, slice(None)), dqb_local)
+    keep_dkv = Bounce(dkv_own, dkv_bounce, dkv_place(dkv.me, slice(None)), dkv_local)
+    load_dy = pltpu.make_async_copy(dy_ref, dy_buf, load_sem.at[0])
+    load_r = pltpu.make_async_copy(r_ref, r_buf, load_sem.at[1])
+    takes = [pltpu.make_async_copy(dkv_ref.at[t * short:(t + 1) * short, :], dkv_buf.at[t], dkv_sem.at[t]) for t in range(dkv_buf.shape[0])]
+
+    @at_step(0)
+    def _():
+        load_dy.start()
+        greet(seq_par)
+        dkv.start()
+        keep_dqb.fetch.start()
+        keep_dkv.fetch.start()
+        load_dy.wait()
+        load_r.start()
+
+    @at_step(1)
+    def _():
+        keep_dqb.turn()
+        keep_dkv.turn()
+
+    @at_step(2)
+    def _():
+        dkv.forward()
+        dqb.start()
+
+    @at_step(4)
+    def _():
+        dkv.relay_near()
+
+    @at_step(6)
+    def _():
+        dkv.relay_far()
+
+    @at_step(TILES)
+    def _():
+        dqb.forward()
+        load_r.wait()
+        keep_dkv.keep.wait()
+        dkv.finish_recvs()
+        for take in takes:
+            take.start()
+
+    @at_step(TILES + 2)
+    def _():
+        dqb.relay_near()
+
+    @pl.when(tile < TILES)
+    def _():
+        dwo_ref[...] = dot(o_ref[...], dy_buf[...])
+
+    for t, take in enumerate(takes):
+        @at_step(TILES + t)
+        def _(take=take):
+            take.wait()
+
+    @pl.when(tile >= TILES)
+    def _():
+        both = dot(dkv_buf[tile - TILES], r_buf[...])
+        for h in range(dk_ref.shape[0] // dim):
+            dk_ref[h * dim:(h + 1) * dim, :] = both[2 * h * dim:(2 * h + 1) * dim, :]
+            dv_ref[h * dim:(h + 1) * dim, :] = both[(2 * h + 1) * dim:(2 * h + 2) * dim, :]
+
+    @pl.when(tile == pl.num_programs(0) - 1)
+    def _():
+        dqb.relay_far()
+        keep_dqb.keep.wait()
+        dqb.finish_recvs()
+        dqb.finish_sends()
+        dkv.finish_sends()
+
+
+TILES = 8
+
+
+def tail_gather(o_all, dy_all, normed_all, dqb_t, dkv_t, dim, seq_par):
+    rows, seq = o_all.shape
+    d_model = dy_all.shape[1]
+    pair_rows = dkv_t.shape[0] * seq_par
+    tall = rows // TILES
+    short = math.gcd(pair_rows, 256)
+    hbm = pl.BlockSpec(memory_space=pl.ANY)
+    first = lambda i: (jnp.minimum(i, TILES - 1), 0)
+    second = lambda i: (jnp.maximum(i - TILES, 0), 0)
     return pl.pallas_call(
-        outer_kernel,
-        grid=(rows // tall,),
-        in_specs=[pl.BlockSpec((tall, p.shape[1]), lambda m: (m, 0)) for p in parts] + [pl.BlockSpec((depth, d_model), lambda m: (0, 0))],
-        out_specs=pl.BlockSpec((tall, d_model), lambda m: (m, 0)),
-        out_shape=jax.ShapeDtypeStruct((rows, d_model), F32),
+        functools.partial(tail_gather_kernel, seq_par, dim),
+        grid=(TILES + pair_rows // short,),
+        in_specs=[pl.BlockSpec((tall, seq), first), hbm, hbm, hbm, hbm],
+        out_specs=[pl.BlockSpec((tall, d_model), first), pl.BlockSpec((short // 2, d_model), second), pl.BlockSpec((short // 2, d_model), second), hbm, hbm],
+        out_shape=[
+            jax.ShapeDtypeStruct((rows, d_model), F32),
+            jax.ShapeDtypeStruct((pair_rows // 2, d_model), F32),
+            jax.ShapeDtypeStruct((pair_rows // 2, d_model), F32),
+            jax.ShapeDtypeStruct((dqb_t.shape[0] * seq_par, dqb_t.shape[1]), BF16),
+            jax.ShapeDtypeStruct((pair_rows, seq), BF16),
+        ],
+        scratch_shapes=[
+            pltpu.VMEM(dy_all.shape, BF16),
+            pltpu.VMEM(normed_all.shape, BF16),
+            pltpu.VMEM((pair_rows // short, short, seq), BF16),
+            pltpu.SemaphoreType.DMA((2,)),
+            pltpu.SemaphoreType.DMA((pair_rows // short,)),
+            pltpu.VMEM(dqb_t.shape, BF16),
+            pltpu.VMEM(dkv_t.shape, BF16),
+            pltpu.SemaphoreType.DMA((2,)),
+            pltpu.SemaphoreType.DMA((2,)),
+        ] + GATHER_SEMS + GATHER_SEMS,
+        compiler_params=pltpu.CompilerParams(collective_id=5, has_side_effects=True, vmem_limit_bytes=60 << 20),
+        cost_estimate=pl.CostEstimate(flops=2 * d_model * seq * (rows + pair_rows), transcendentals=0, bytes_accessed=8 * rows * d_model),
+        name='tail_gather',
+    )(o_all, dy_all, normed_all, dqb_t, dkv_t)
+
+
+def finish_kernel(dqa_ref, dqb_ref, dwo_in, dk_in, dv_in, y_in, dx_in, r_ref, dwq_ref, dwo_ref, dk_ref, dv_ref, y_ref, dx_ref, r_buf, load_sem):
+    half = dqa_ref.shape[1]
+    early = pltpu.make_async_copy(r_ref.at[:half, :], r_buf.at[:half, :], load_sem.at[0])
+    late = pltpu.make_async_copy(r_ref.at[half:, :], r_buf.at[half:, :], load_sem.at[1])
+
+    @at_step(0)
+    def _():
+        early.start()
+        late.start()
+
+    def hand_on():
+        dwo_ref[...] = dwo_in[...]
+        dk_ref[...] = dk_in[...]
+        dv_ref[...] = dv_in[...]
+        y_ref[...] = y_in[...]
+        dx_ref[...] = dx_in[...]
+
+    @at_step(0)
+    def _():
+        hand_on()
+        early.wait()
+        dwq_ref[...] = dot(dqa_ref[...], r_buf[:half, :])
+        late.wait()
+        dwq_ref[...] += dot(dqb_ref[...], r_buf[half:, :])
+
+    @pl.when(pl.program_id(0) > 0)
+    def _():
+        hand_on()
+        dwq_ref[...] = dot(dqa_ref[...], r_buf[:half, :]) + dot(dqb_ref[...], r_buf[half:, :])
+
+
+def finish_grads(dqa_all, dqb_all, passed, normed_all):
+    rows, half = dqa_all.shape
+    seq, d_model = normed_all.shape
+    band = lambda a: pl.BlockSpec((a.shape[0] // TILES, a.shape[1]), lambda i: (i, 0))
+    out = jax.ShapeDtypeStruct((rows, d_model), F32)
+    return pl.pallas_call(
+        finish_kernel,
+        grid=(TILES,),
+        in_specs=[band(dqa_all), band(dqb_all)] + [band(p) for p in passed] + [pl.BlockSpec(memory_space=pl.ANY)],
+        out_specs=[band(out)] + [band(p) for p in passed],
+        out_shape=[out] + [jax.ShapeDtypeStruct(p.shape, p.dtype) for p in passed],
+        scratch_shapes=[pltpu.VMEM(normed_all.shape, BF16), pltpu.SemaphoreType.DMA((2,))],
         compiler_params=pltpu.CompilerParams(vmem_limit_bytes=60 << 20),
-        cost_estimate=pl.CostEstimate(flops=2 * rows * depth * d_model, transcendentals=0, bytes_accessed=2 * depth * (rows + d_model) + 4 * rows * d_model),
-        name=name,
-    )(*parts, rhs)
-
-
-def pair_kernel(dim, lhs_ref, rhs_ref, dk_ref, dv_ref):
-    both = dot(lhs_ref[...], rhs_ref[...])
-    for h in range(dk_ref.shape[0] // dim):
-        dk_ref[h * dim:(h + 1) * dim, :] = both[2 * h * dim:(2 * h + 1) * dim, :]
-        dv_ref[h * dim:(h + 1) * dim, :] = both[(2 * h + 1) * dim:(2 * h + 2) * dim, :]
-
-
-def pair_grad(lhs, rhs, dim):
-    rows, depth = lhs.shape
-    d_model = rhs.shape[1]
-    tall = math.gcd(rows, 256)
-    out = pl.BlockSpec((tall // 2, d_model), lambda m: (m, 0))
-    return pl.pallas_call(
-        functools.partial(pair_kernel, dim),
-        grid=(rows // tall,),
-        in_specs=[pl.BlockSpec((tall, depth), lambda m: (m, 0)), pl.BlockSpec((depth, d_model), lambda m: (0, 0))],
-        out_specs=[out, out],
-        out_shape=[jax.ShapeDtypeStruct((rows // 2, d_model), F32)] * 2,
-        compiler_params=pltpu.CompilerParams(vmem_limit_bytes=60 << 20),
-        cost_estimate=pl.CostEstimate(flops=2 * rows * depth * d_model, transcendentals=0, bytes_accessed=2 * depth * (rows + d_model) + 4 * rows * d_model),
-        name='d_wkv',
-    )(lhs, rhs)
+        cost_estimate=pl.CostEstimate(flops=2 * d_model * rows * seq, transcendentals=0, bytes_accessed=16 * rows * d_model),
+        name='finish_grads',
+    )(dqa_all, dqb_all, *passed, normed_all)
 
 
 def input_grad_kernel(seq_par, dqa_ref, dqb_ref, dkv_ref, wq_ref, wk_ref, wv_ref, x_ref, dy_ref, gain_ref, dx_ref, dgain_ref, dq_buf, dk_buf, dv_buf, wq_buf, wk_buf, wv_buf, acc, part, slots, act_sem, w_sem, send_sem, recv_sem):
@@ -586,14 +680,14 @@
     inv_rms = lax.rsqrt(jnp.mean(x_f32 * x_f32, axis=-1, keepdims=True) + NORM_EPS)
     part[...] = jnp.sum(d_normed * (x_f32 * inv_rms), axis=0, keepdims=True)
     dots = jnp.mean(acc[...] * gain_ref[...] * (x_ref[...].astype(F32) * inv_rms), axis=-1, keepdims=True)
-    x_hat = x_ref[...].astype(F32) * inv_rms
-    dx_ref[...] = (dy_ref[...].astype(F32) + inv_rms * (acc[...] * gain_ref[...] - x_hat * dots)).astype(BF16)
     pl.semaphore_wait(barrier, seq_par - 1)
     copies = []
     for step in range(1, seq_par):
         copies.append(pltpu.make_async_remote_copy(src_ref=part, dst_ref=slots.at[me], send_sem=send_sem.at[step], recv_sem=recv_sem.at[step], device_id={'sp': lax.rem(me + step, seq_par)}, device_id_type=pl.DeviceIdType.MESH))
         copies[-1].start()
     slots[me] = part[...]
+    x_hat = x_ref[...].astype(F32) * inv_rms
+    dx_ref[...] = (dy_ref[...].astype(F32) + inv_rms * (acc[...] * gain_ref[...] - x_hat * dots)).astype(BF16)
     for copy in copies:
         copy.wait_recv()
     total = slots[0]
@@ -653,21 +747,13 @@
         wk_t = jnp.transpose(w_k, (1, 2, 0)).reshape(num_kv * dim, d_model)
         wv_t = jnp.transpose(w_v, (1, 2, 0)).reshape(num_kv * dim, d_model)
         wo_t = w_o.reshape(num_q * dim, d_model)
-        gather = lambda a: lax.all_gather(a, 'sp', axis=0, tiled=True)
 
         cos_t, sin_t = rope_tables(jnp.arange(seq, dtype=F32), dim)
-        normed = norm_forward(x_local, gain)
-        normed_all, q_t, k_t, v_t, k_rows, v_rows = gather_project(normed, wq_t, wk_t, wv_t, cos_t, sin_t, group, seq_par)
-        o_t, lse, dy_all = attention_forward(q_t, k_rows, v_t, dy_local, group, seq_par)
+        normed_all, q_t, k_t, k_rows, v_rows, o_t, lse, dy_all = attention_forward(x_local, gain, wq_t, wk_t, wv_t, cos_t, sin_t, dy_local, group, seq_par)
         dqb_t, dkv_t, y_out, o_all, dqa_all = attention_backward(x_local, q_t, dy_all, wo_t, o_t, lse, k_rows, v_rows, k_t, cos_t, sin_t, group, seq_par)
-        dqb_all = gather(dqb_t)
-        d_wo = weight_grad([o_all], dy_all, 'd_wo')
-        dkv_t, d_wo = lax.optimization_barrier((dkv_t, d_wo))
-        dkv_all = gather(dkv_t)
-        d_wq = weight_grad([dqa_all, dqb_all], normed_all, 'd_wq')
-        dkv_all, d_wq = lax.optimization_barrier((dkv_all, d_wq))
-        d_wk, d_wv = pair_grad(dkv_all, normed_all, dim)
+        d_wo, d_wk, d_wv, dqb_all, dkv_all = tail_gather(o_all, dy_all, normed_all, dqb_t, dkv_t, dim, seq_par)
         d_x, d_gain = input_grad(dqa_all, dqb_all, dkv_all, wq_t, wk_t, wv_t, x_local, dy_local, gain, dim, seq_par)
+        d_wq, d_wo, d_wk, d_wv, y_out, d_x = finish_grads(dqa_all, dqb_all, [d_wo, d_wk, d_wv, y_out, d_x], normed_all)
         unflat = lambda g, heads: jnp.transpose(g.reshape(heads, dim, d_model), (2, 0, 1))
         return y_out[None], d_x[None], unflat(d_wq, num_q), unflat(d_wk, num_kv), unflat(d_wv, num_kv), d_wo.reshape(num_q, dim, d_model), d_gain[0]
 

time: 351 us -> 330 us (0.940)
  between operations: 14.3 us -> 0.69 us
  Pallas kernels: 314 us -> 326 us
  waiting for transfers between devices: 11.4 us -> 0 us
  local copies, waits for them, and re-layouts: 5.49 us -> 0.61 us
    pallas_call x1, Pallas kernels: 58.3 us -> 121 us  [attention_forward(): pl.pallas_call(functools.partial(forward_kernel, seq_par, group, scale),...]
    pallas_call x4 -> x2, Pallas kernels: 150 us -> 101 us  [the longest x1 60.5 us: tail_gather(): pl.pallas_call(functools.partial(tail_gather_kernel, seq_par, dim), grid=...]
    all_gather x2 -> x0, waiting for transfers between devices: 11.3 us -> none  [local_step(): gather = lambda a: lax.all_gather(a, 'sp', axis=0, tiled=True)]
    unnamed x29 -> x3, local copies, waits for them, and re-layouts: 5.49 us -> 0.61 us
  transfers between devices with their start and end apart: 2 -> 0, of which waited for: 2 -> 0; matrix products, arithmetic and copies ran while one was open for 0% -> 0% of each run, Pallas kernels for 19% -> 0%
where the time goes in v3:
time: 330 us
  Pallas kernels  326 us (99%)
    pallas_call x1, Pallas kernels, attention_forward(): pl.pallas_call(functools.partial(forward_kernel, seq_par, group, scale),...  121 us
    pallas_call x1, Pallas kernels, attention_backward(): pl.pallas_call(functools.partial(backward_kernel, seq_par, group, scale),...  89.2 us
    pallas_call x1, Pallas kernels, tail_gather(): pl.pallas_call(functools.partial(tail_gather_kernel, seq_par, dim), grid=...  60.5 us
    pallas_call x1, Pallas kernels, finish_grads(): pl.pallas_call(finish_kernel, grid=(TILES,), in_specs=[band(dqa_all), ban...  40.7 us
    pallas_call x1, Pallas kernels, input_grad(): pl.pallas_call(functools.partial(input_grad_kernel, seq_par), in_specs=[h...  15.3 us

profile of v3, /device:TPU:81, one launch (start us, length us, event | category | flops | bytes accessed | tf_op | source)
XLA Modules:
  0.0 330.0 jit_solution(4196457786851141310)
XLA Ops:
  0.6 2.3 fusion
  3.0 120.7 %attn_fwd.1 = (bf16[3072,2048]{1,0:T(8,128)(2,1)}, bf16[256,3072]{1,0:T(8,128)(2,1)}, bf16[64,3072]{1,0:T(8,128)(2,1)}, bf16[3072,64]{1,0:T(8,128)(2,1)}, bf16[3...) custom-call(bf16[384,2048]{1,0:T(8,128)(2,1)} %bitcast.34, ...), custom_call_target="tpu_custom_call" | custom-call | flops 20937965568 | bytes 50331648 | tf_op jit(solution)/shard_map/attn_fwd/pallas_call | solution.py:298
  123.7 89.2 %attn_bwd.1 = (bf16[256,1536]{1,0:T(8,128)(2,1)}, bf16[128,3072]{1,0:T(8,128)(2,1)}, bf16[384,2048]{1,0:T(8,128)(2,1)}, bf16[2048,3072]{1,0:T(8,128)(2,1)}, bf16[2048,1536]{1,0:T(8,128)(2,1)}) custom-call(bf16[256,3072]{1,0:T(8,128)(2,1)} %get-tuple-element.33.q_ref, bf16[3072,2048]{1,0:T(8,128)(2,1)} %get-tuple-element.34.dy_ref, ...), custom_call_target="tpu_custom_call" | custom-call | flops 52344913920 | bytes 9437184 | tf_op jit(solution)/shard_map/attn_bwd/pallas_call | solution.py:444
  212.9 60.5 %tail_gather.1 = (f32[2048,2048]{1,0:T(8,128)}, f32[512,2048]{1,0:T(8,128)}, f32[512,2048]{1,0:T(8,128)}, bf16[2048,1536]{1,0:T(8,128)(2,1)}, bf16[1024,3072]{1,0:T(8,128)(2,1)}) custom-call(bf16[2048,3072]{1,0:T(8,128)(2,1)} %get-tuple-element.41.o_ref, bf16[3072,2048]{1,0:T(8,128)(2,1)} %get-tuple-element.34.dy_ref, ...), custom_call_target="tpu_custom_call" | custom-call | flops 38654705664 | bytes 33554432 | tf_op jit(solution)/shard_map/tail_gather/pallas_call | solution.py:554
  273.4 15.3 %input_grad.1 = (bf16[384,2048]{1,0:T(8,128)(2,1)}, f32[1,2048]{1,0:T(1,128)}) custom-call(bf16[2048,1536]{1,0:T(8,128)(2,1)} %get-tuple-element.40.dqa_ref, bf16[2048,1536]{1,0:T(8,128)(2,1)} %get-tuple-element.45.dqb_ref, bf16[8,2,64,3072]{3,2,1,0:T(8,128)(2,1)} %bitcast.29, bf16[2048,2048]{1,0:T(8,128)(2,1)} %bitcast.28, bf16[512,2048]{1,0:T(8,128)(2,1)} %bitcast.31, ...), custom_call_target="tpu_custom_call" | custom-call | flops 4831838208 | bytes 12582912 | tf_op jit(solution)/shard_map/input_grad/pallas_call | solution.py:707
  288.7 0.0 copy-start
  288.7 40.7 %finish_grads.1 = (f32[2048,2048]{1,0:T(8,128)}, f32[2048,2048]{1,0:T(8,128)}, f32[512,2048]{1,0:T(8,128)}, f32[512,2048]{1,0:T(8,128)}, bf16[384,2048]{1,0:T(8,128)(2,1)}, /*index=5*/bf16[384,2048]{1,0:T(8,128)(2,1)}) custom-call(bf16[2048,1536]{1,0:T(8,128)(2,1)} %get-tuple-element.40.dqa_ref, bf16[2048,1536]{1,0:T(8,128)(2,1)} %get-tuple-element.45.dqb_ref, ...), custom_call_target="tpu_custom_call" | custom-call | flops 25769803776 | bytes 67108864 | tf_op jit(solution)/shard_map/finish_grads/pallas_call | solution.py:619
  329.4 0.0 copy-done
  329.4 0.6 copy.15
  (1 shorter events, 0.0 us)
Async XLA Ops:
  288.7 40.7 %copy-start = (f32[1,2048]{1,0:T(1,128)S(1)}, f32[1,2048]{1,0:T(1,128)}, u32[]{:S(2)}) copy-start(f32[1,2048]{1,0:T(1,128)} %get-tuple-element.58) | copy-start | bytes 24580

commit v4 on v3

--- a/solution.py
+++ b/solution.py
@@ -127,6 +127,14 @@
     if meanwhile is not None:
         meanwhile()
     pl.semaphore_wait(barrier, 3)
+
+
+def greet_all(seq_par):
+    me = lax.axis_index('sp')
+    barrier = pltpu.get_barrier_semaphore()
+    for step in range(1, seq_par):
+        pl.semaphore_signal(barrier, inc=1, device_id={'sp': lax.rem(me + step, seq_par)}, device_id_type=pl.DeviceIdType.MESH)
+    pl.semaphore_wait(barrier, seq_par - 1)
 
 
 def row_place(ref, rows):
@@ -460,7 +468,7 @@
     )(q_t, dy_all, wo_t, o_t, lse, k_rows, v_rows, k_t, cos_t, sin_t, o_t, x_local)
 
 
-def tail_gather_kernel(seq_par, dim, o_ref, dy_ref, r_ref, dqb_own, dkv_own, dwo_ref, dk_ref, dv_ref, dqb_ref, dkv_ref, dy_buf, r_buf, dkv_buf, load_sem, dkv_sem, dqb_bounce, dkv_bounce, dqb_local, dkv_local, dqb_send, dqb_recv, dkv_send, dkv_recv):
+def tail_gather_kernel(seq_par, dim, o_ref, dy_ref, r_ref, dqb_own, dkv_own, dqa_ref, wq_ref, wk_ref, wv_ref, x_ref, dyl_ref, gain_ref, dwo_ref, dk_ref, dv_ref, dqb_ref, dkv_ref, dx_ref, dgain_ref, dy_buf, r_buf, dkv_buf, load_sem, dkv_sem, dqb_bounce, dkv_bounce, dqb_local, dkv_local, dqb_send, dqb_recv, dkv_send, dkv_recv, dq_buf, acc, part, slots, w_sem, dq_sem, gain_send, gain_recv):
     tile = pl.program_id(0)
     short = dkv_buf.shape[1]
     dqb_place = row_place(dqb_ref, dqb_own.shape[0])
@@ -473,10 +481,20 @@
     load_r = pltpu.make_async_copy(r_ref, r_buf, load_sem.at[1])
     takes = [pltpu.make_async_copy(dkv_ref.at[t * short:(t + 1) * short, :], dkv_buf.at[t], dkv_sem.at[t]) for t in range(dkv_buf.shape[0])]
 
+    me = dqb.me
+    tokens = x_ref.shape[0]
+    half = dqa_ref.shape[1]
+    ends = [wq_ref.shape[0], wq_ref.shape[0] + wk_ref.shape[0]]
+    weights = [
+        pltpu.make_async_copy(wq_ref, dy_buf.at[:ends[0], :], w_sem.at[0]),
+        pltpu.make_async_copy(wk_ref, dy_buf.at[ends[0]:ends[1], :], w_sem.at[1]),
+        pltpu.make_async_copy(wv_ref, dy_buf.at[ends[1]:, :], w_sem.at[2]),
+    ]
+
     @at_step(0)
     def _():
         load_dy.start()
-        greet(seq_par)
+        greet_all(seq_par)
         dkv.start()
         keep_dqb.fetch.start()
         keep_dkv.fetch.start()
@@ -509,6 +527,8 @@
         dkv.finish_recvs()
         for take in takes:
             take.start()
+        for copy in weights:
+            copy.start()
 
     @at_step(TILES + 2)
     def _():
@@ -532,9 +552,55 @@
 
     @pl.when(tile == pl.num_programs(0) - 1)
     def _():
+        for copy in weights:
+            copy.wait()
+        cols = pl.ds(pl.multiple_of(me * tokens, tokens), tokens)
+        per = short // (2 * dim)
+        heads = [(t, 2 * h * dim) for t in range(dkv_buf.shape[0]) for h in range(per)]
+        dk_mine = jnp.concatenate([dkv_buf[t, start:start + dim, cols] for t, start in heads], axis=0)
+        dv_mine = jnp.concatenate([dkv_buf[t, start + dim:start + 2 * dim, cols] for t, start in heads], axis=0)
+        acc[...] = dot(dk_mine.T, dy_buf[ends[0]:ends[1], :])
+        acc[...] += dot(dv_mine.T, dy_buf[ends[1]:, :])
         dqb.relay_far()
         keep_dqb.keep.wait()
         dqb.finish_recvs()
+        low = me * tokens < half
+        first = pl.multiple_of(jnp.where(low, me * tokens, 0), 128)
+        second = pl.multiple_of(jnp.where(low, 0, me * tokens - half), 128)
+        from_a = pltpu.make_async_copy(dqa_ref.at[:, pl.ds(first, tokens)], dq_buf, dq_sem)
+        from_b = pltpu.make_async_copy(dqb_ref.at[:, pl.ds(second, tokens)], dq_buf, dq_sem)
+
+        @pl.when(low)
+        def _():
+            from_a.start()
+
+        @pl.when(jnp.logical_not(low))
+        def _():
+            from_b.start()
+
+        from_a.wait()
+        acc[...] += dot(dq_buf[...].T, dy_buf[:ends[0], :])
+        d_normed = acc[...].astype(BF16).astype(F32)
+        acc[...] = d_normed
+        x_f32 = x_ref[...].astype(F32)
+        inv_rms = lax.rsqrt(jnp.mean(x_f32 * x_f32, axis=-1, keepdims=True) + NORM_EPS)
+        part[...] = jnp.sum(d_normed * (x_f32 * inv_rms), axis=0, keepdims=True)
+        dots = jnp.mean(acc[...] * gain_ref[...] * (x_ref[...].astype(F32) * inv_rms), axis=-1, keepdims=True)
+        copies = []
+        for step in range(1, seq_par):
+            copies.append(pltpu.make_async_remote_copy(src_ref=part, dst_ref=slots.at[me], send_sem=gain_send.at[step], recv_sem=gain_recv.at[step], device_id={'sp': lax.rem(me + step, seq_par)}, device_id_type=pl.DeviceIdType.MESH))
+            copies[-1].start()
+        slots[me] = part[...]
+        x_hat = x_ref[...].astype(F32) * inv_rms
+        dx_ref[...] = (dyl_ref[...].astype(F32) + inv_rms * (acc[...] * gain_ref[...] - x_hat * dots)).astype(BF16)
+        for copy in copies:
+            copy.wait_recv()
+        total = slots[0]
+        for step in range(1, seq_par):
+            total = total + slots[step]
+        dgain_ref[...] = total
+        for copy in copies:
+            copy.wait_send()
         dqb.finish_sends()
         dkv.finish_sends()
 
@@ -542,26 +608,32 @@
 TILES = 8
 
 
-def tail_gather(o_all, dy_all, normed_all, dqb_t, dkv_t, dim, seq_par):
+def tail_gather(o_all, dy_all, normed_all, dqb_t, dkv_t, dqa_all, wq_t, wk_t, wv_t, x_local, dy_local, gain, dim, seq_par):
     rows, seq = o_all.shape
     d_model = dy_all.shape[1]
     pair_rows = dkv_t.shape[0] * seq_par
     tall = rows // TILES
     short = math.gcd(pair_rows, 256)
     hbm = pl.BlockSpec(memory_space=pl.ANY)
+    tokens = x_local.shape[0]
+    if wq_t.shape[0] + 2 * wk_t.shape[0] != seq:
+        raise ValueError('unsupported shapes')
+    whole = lambda shape: pl.BlockSpec(shape, lambda i: (0, 0))
     first = lambda i: (jnp.minimum(i, TILES - 1), 0)
     second = lambda i: (jnp.maximum(i - TILES, 0), 0)
     return pl.pallas_call(
         functools.partial(tail_gather_kernel, seq_par, dim),
         grid=(TILES + pair_rows // short,),
-        in_specs=[pl.BlockSpec((tall, seq), first), hbm, hbm, hbm, hbm],
-        out_specs=[pl.BlockSpec((tall, d_model), first), pl.BlockSpec((short // 2, d_model), second), pl.BlockSpec((short // 2, d_model), second), hbm, hbm],
+        in_specs=[pl.BlockSpec((tall, seq), first)] + [hbm] * 8 + [whole(x_local.shape), whole(x_local.shape), whole((1, d_model))],
+        out_specs=[pl.BlockSpec((tall, d_model), first), pl.BlockSpec((short // 2, d_model), second), pl.BlockSpec((short // 2, d_model), second), hbm, hbm, whole(x_local.shape), whole((1, d_model))],
         out_shape=[
             jax.ShapeDtypeStruct((rows, d_model), F32),
             jax.ShapeDtypeStruct((pair_rows // 2, d_model), F32),
             jax.ShapeDtypeStruct((pair_rows // 2, d_model), F32),
             jax.ShapeDtypeStruct((dqb_t.shape[0] * seq_par, dqb_t.shape[1]), BF16),
             jax.ShapeDtypeStruct((pair_rows, seq), BF16),
+            jax.ShapeDtypeStruct(x_local.shape, BF16),
+            jax.ShapeDtypeStruct((1, d_model), F32),
         ],
         scratch_shapes=[
             pltpu.VMEM(dy_all.shape, BF16),
@@ -573,11 +645,20 @@
             pltpu.VMEM(dkv_t.shape, BF16),
             pltpu.SemaphoreType.DMA((2,)),
             pltpu.SemaphoreType.DMA((2,)),
-        ] + GATHER_SEMS + GATHER_SEMS,
-        compiler_params=pltpu.CompilerParams(collective_id=5, has_side_effects=True, vmem_limit_bytes=60 << 20),
+        ] + GATHER_SEMS + GATHER_SEMS + [
+            pltpu.VMEM((wq_t.shape[0], tokens), BF16),
+            pltpu.VMEM((tokens, d_model), F32),
+            pltpu.VMEM((1, d_model), F32),
+            pltpu.VMEM((seq_par, 1, d_model), F32),
+            pltpu.SemaphoreType.DMA((3,)),
+            pltpu.SemaphoreType.DMA,
+            pltpu.SemaphoreType.DMA((seq_par,)),
+            pltpu.SemaphoreType.DMA((seq_par,)),
+        ],
+        compiler_params=pltpu.CompilerParams(collective_id=5, has_side_effects=True, vmem_limit_bytes=63 << 20),
         cost_estimate=pl.CostEstimate(flops=2 * d_model * seq * (rows + pair_rows), transcendentals=0, bytes_accessed=8 * rows * d_model),
         name='tail_gather',
-    )(o_all, dy_all, normed_all, dqb_t, dkv_t)
+    )(o_all, dy_all, normed_all, dqb_t, dkv_t, dqa_all, wq_t, wk_t, wv_t, x_local, dy_local, gain[None])
 
 
 def finish_kernel(dqa_ref, dqb_ref, dwo_in, dk_in, dv_in, y_in, dx_in, r_ref, dwq_ref, dwo_ref, dk_ref, dv_ref, y_ref, dx_ref, r_buf, load_sem):
@@ -629,107 +710,6 @@
     )(dqa_all, dqb_all, *passed, normed_all)
 
 
-def input_grad_kernel(seq_par, dqa_ref, dqb_ref, dkv_ref, wq_ref, wk_ref, wv_ref, x_ref, dy_ref, gain_ref, dx_ref, dgain_ref, dq_buf, dk_buf, dv_buf, wq_buf, wk_buf, wv_buf, acc, part, slots, act_sem, w_sem, send_sem, recv_sem):
-    me = lax.axis_index('sp')
-    tokens, d_model = x_ref.shape
-    half = dqa_ref.shape[1]
-    barrier = pltpu.get_barrier_semaphore()
-    for step in range(1, seq_par):
-        pl.semaphore_signal(barrier, inc=1, device_id={'sp': lax.rem(me + step, seq_par)}, device_id_type=pl.DeviceIdType.MESH)
-    low = me * tokens < half
-    first = pl.multiple_of(jnp.where(low, me * tokens, 0), 128)
-    second = pl.multiple_of(jnp.where(low, 0, me * tokens - half), 128)
-    cols = pl.ds(pl.multiple_of(me * tokens, tokens), tokens)
-    from_a = pltpu.make_async_copy(dqa_ref.at[:, pl.ds(first, tokens)], dq_buf, act_sem.at[0])
-    from_b = pltpu.make_async_copy(dqb_ref.at[:, pl.ds(second, tokens)], dq_buf, act_sem.at[0])
-
-    @pl.when(low)
-    def _():
-        from_a.start()
-
-    @pl.when(jnp.logical_not(low))
-    def _():
-        from_b.start()
-
-    take_k = pltpu.make_async_copy(dkv_ref.at[:, 0, :, cols], dk_buf, act_sem.at[1])
-    take_v = pltpu.make_async_copy(dkv_ref.at[:, 1, :, cols], dv_buf, act_sem.at[2])
-    take_k.start()
-    take_v.start()
-    chunk = wq_buf.shape[0] // 4
-    loads = [pltpu.make_async_copy(wq_ref.at[c * chunk:(c + 1) * chunk, :], wq_buf.at[c * chunk:(c + 1) * chunk, :], w_sem.at[c]) for c in range(4)]
-    loads += [pltpu.make_async_copy(wk_ref, wk_buf, w_sem.at[4]), pltpu.make_async_copy(wv_ref, wv_buf, w_sem.at[5])]
-    for copy in loads:
-        copy.start()
-    from_a.wait()
-    for c in range(4):
-        loads[c].wait()
-        term = dot(dq_buf[c * chunk:(c + 1) * chunk, :].T, wq_buf[c * chunk:(c + 1) * chunk, :])
-        if c == 0:
-            acc[...] = term
-        else:
-            acc[...] += term
-    take_k.wait()
-    take_v.wait()
-    loads[4].wait()
-    loads[5].wait()
-    acc[...] += dot(dk_buf[...].reshape(wk_buf.shape[0], tokens).T, wk_buf[...])
-    acc[...] += dot(dv_buf[...].reshape(wv_buf.shape[0], tokens).T, wv_buf[...])
-    d_normed = acc[...].astype(BF16).astype(F32)
-    acc[...] = d_normed
-    x_f32 = x_ref[...].astype(F32)
-    inv_rms = lax.rsqrt(jnp.mean(x_f32 * x_f32, axis=-1, keepdims=True) + NORM_EPS)
-    part[...] = jnp.sum(d_normed * (x_f32 * inv_rms), axis=0, keepdims=True)
-    dots = jnp.mean(acc[...] * gain_ref[...] * (x_ref[...].astype(F32) * inv_rms), axis=-1, keepdims=True)
-    pl.semaphore_wait(barrier, seq_par - 1)
-    copies = []
-    for step in range(1, seq_par):
-        copies.append(pltpu.make_async_remote_copy(src_ref=part, dst_ref=slots.at[me], send_sem=send_sem.at[step], recv_sem=recv_sem.at[step], device_id={'sp': lax.rem(me + step, seq_par)}, device_id_type=pl.DeviceIdType.MESH))
-        copies[-1].start()
-    slots[me] = part[...]
-    x_hat = x_ref[...].astype(F32) * inv_rms
-    dx_ref[...] = (dy_ref[...].astype(F32) + inv_rms * (acc[...] * gain_ref[...] - x_hat * dots)).astype(BF16)
-    for copy in copies:
-        copy.wait_recv()
-    total = slots[0]
-    for step in range(1, seq_par):
-        total = total + slots[step]
-    dgain_ref[...] = total
-    for copy in copies:
-        copy.wait_send()
-
-
-def input_grad(dqa_all, dqb_all, dkv_all, wq_t, wk_t, wv_t, x_local, dy_local, gain, dim, seq_par):
-    tokens, d_model = x_local.shape
-    num_kv = wk_t.shape[0] // dim
-    seq = dkv_all.shape[1]
-    vmem = pl.BlockSpec(memory_space=pltpu.VMEM)
-    hbm = pl.BlockSpec(memory_space=pl.ANY)
-    return pl.pallas_call(
-        functools.partial(input_grad_kernel, seq_par),
-        in_specs=[hbm] * 6 + [vmem] * 3,
-        out_specs=[vmem, vmem],
-        out_shape=[jax.ShapeDtypeStruct(x_local.shape, BF16), jax.ShapeDtypeStruct((1, d_model), F32)],
-        scratch_shapes=[
-            pltpu.VMEM((wq_t.shape[0], tokens), BF16),
-            pltpu.VMEM((num_kv, dim, tokens), BF16),
-            pltpu.VMEM((num_kv, dim, tokens), BF16),
-            pltpu.VMEM(wq_t.shape, BF16),
-            pltpu.VMEM(wk_t.shape, BF16),
-            pltpu.VMEM(wv_t.shape, BF16),
-            pltpu.VMEM((tokens, d_model), F32),
-            pltpu.VMEM((1, d_model), F32),
-            pltpu.VMEM((seq_par, 1, d_model), F32),
-            pltpu.SemaphoreType.DMA((3,)),
-            pltpu.SemaphoreType.DMA((6,)),
-            pltpu.SemaphoreType.DMA((seq_par,)),
-            pltpu.SemaphoreType.DMA((seq_par,)),
-        ],
-        compiler_params=pltpu.CompilerParams(collective_id=4, has_side_effects=True, vmem_limit_bytes=56 << 20),
-        cost_estimate=pl.CostEstimate(flops=2 * tokens * d_model * (wq_t.shape[0] + 2 * wk_t.shape[0]), transcendentals=0, bytes_accessed=2 * d_model * (wq_t.shape[0] + 2 * wk_t.shape[0])),
-        name='input_grad',
-    )(dqa_all, dqb_all, dkv_all.reshape(num_kv, 2, dim, seq), wq_t, wk_t, wv_t, x_local, dy_local, gain[None])
-
-
 def solution(mesh):
     seq_par = mesh.shape['sp']
 
@@ -751,8 +731,7 @@
         cos_t, sin_t = rope_tables(jnp.arange(seq, dtype=F32), dim)
         normed_all, q_t, k_t, k_rows, v_rows, o_t, lse, dy_all = attention_forward(x_local, gain, wq_t, wk_t, wv_t, cos_t, sin_t, dy_local, group, seq_par)
         dqb_t, dkv_t, y_out, o_all, dqa_all = attention_backward(x_local, q_t, dy_all, wo_t, o_t, lse, k_rows, v_rows, k_t, cos_t, sin_t, group, seq_par)
-        d_wo, d_wk, d_wv, dqb_all, dkv_all = tail_gather(o_all, dy_all, normed_all, dqb_t, dkv_t, dim, seq_par)
-        d_x, d_gain = input_grad(dqa_all, dqb_all, dkv_all, wq_t, wk_t, wv_t, x_local, dy_local, gain, dim, seq_par)
+        d_wo, d_wk, d_wv, dqb_all, _, d_x, d_gain = tail_gather(o_all, dy_all, normed_all, dqb_t, dkv_t, dqa_all, wq_t, wk_t, wv_t, x_local, dy_local, gain, dim, seq_par)
         d_wq, d_wo, d_wk, d_wv, y_out, d_x = finish_grads(dqa_all, dqb_all, [d_wo, d_wk, d_wv, y_out, d_x], normed_all)
         unflat = lambda g, heads: jnp.transpose(g.reshape(heads, dim, d_model), (2, 0, 1))
         return y_out[None], d_x[None], unflat(d_wq, num_q), unflat(d_wk, num_kv), unflat(d_wv, num_kv), d_wo.reshape(num_q, dim, d_model), d_gain[0]

time: 330 us -> 326 us (0.988)
  Pallas kernels: 326 us -> 322 us
    pallas_call x1 -> x0, Pallas kernels: 15.3 us -> none  [input_grad(): pl.pallas_call(functools.partial(input_grad_kernel, seq_par), in_specs=[h...]
    pallas_call x1, Pallas kernels: 60.5 us -> 71.5 us  [tail_gather(): pl.pallas_call(functools.partial(tail_gather_kernel, seq_par, dim), grid=...]
where the time goes in v4:
time: 326 us
  Pallas kernels  322 us (99%)
    pallas_call x1, Pallas kernels, attention_forward(): pl.pallas_call(functools.partial(forward_kernel, seq_par, group, scale),...  121 us
    pallas_call x1, Pallas kernels, attention_backward(): pl.pallas_call(functools.partial(backward_kernel, seq_par, group, scale),...  89.2 us
    pallas_call x1, Pallas kernels, tail_gather(): pl.pallas_call(functools.partial(tail_gather_kernel, seq_par, dim), grid=...  71.5 us
    pallas_call x1, Pallas kernels, finish_grads(): pl.pallas_call(finish_kernel, grid=(TILES,), in_specs=[band(dqa_all), ban...  40.9 us

profile of v4, /device:TPU:81, one launch (start us, length us, event | category | flops | bytes accessed | tf_op | source)
XLA Modules:
  0.0 325.9 jit_solution(17208606099861454281)
XLA Ops:
  0.6 2.3 fusion
  3.0 120.7 %attn_fwd.1 = (bf16[3072,2048]{1,0:T(8,128)(2,1)}, bf16[256,3072]{1,0:T(8,128)(2,1)}, bf16[64,3072]{1,0:T(8,128)(2,1)}, bf16[3072,64]{1,0:T(8,128)(2,1)}, bf16[3...) custom-call(bf16[384,2048]{1,0:T(8,128)(2,1)} %bitcast.34, ...), custom_call_target="tpu_custom_call" | custom-call | flops 20937965568 | bytes 50331648 | tf_op jit(solution)/shard_map/attn_fwd/pallas_call | solution.py:306
  123.7 89.2 %attn_bwd.1 = (bf16[256,1536]{1,0:T(8,128)(2,1)}, bf16[128,3072]{1,0:T(8,128)(2,1)}, bf16[384,2048]{1,0:T(8,128)(2,1)}, bf16[2048,3072]{1,0:T(8,128)(2,1)}, bf16[2048,1536]{1,0:T(8,128)(2,1)}) custom-call(bf16[256,3072]{1,0:T(8,128)(2,1)} %get-tuple-element.32.q_ref, bf16[3072,2048]{1,0:T(8,128)(2,1)} %get-tuple-element.33.dy_ref, ...), custom_call_target="tpu_custom_call" | custom-call | flops 52344913920 | bytes 9437184 | tf_op jit(solution)/shard_map/attn_bwd/pallas_call | solution.py:452
  212.9 71.5 %tail_gather.1 = (f32[2048,2048]{1,0:T(8,128)}, f32[512,2048]{1,0:T(8,128)}, f32[512,2048]{1,0:T(8,128)}, bf16[2048,1536]{1,0:T(8,128)(2,1)}, bf16[1024,3072]{1,...) custom-call(bf16[2048,3072]{1,0:T(8,128)(2,1)} %get-tuple-element.40.o_ref, ...), custom_call_target="tpu_custom_call" | custom-call | flops 38654705664 | bytes 33554432 | tf_op jit(solution)/shard_map/tail_gather/pallas_call | solution.py:624
  284.4 0.0 copy-start
  284.4 40.9 %finish_grads.1 = (f32[2048,2048]{1,0:T(8,128)}, f32[2048,2048]{1,0:T(8,128)}, f32[512,2048]{1,0:T(8,128)}, f32[512,2048]{1,0:T(8,128)}, bf16[384,2048]{1,0:T(8,128)(2,1)}, /*index=5*/bf16[384,2048]{1,0:T(8,128)(2,1)}) custom-call(bf16[2048,1536]{1,0:T(8,128)(2,1)} %get-tuple-element.39.dqa_ref, bf16[2048,1536]{1,0:T(8,128)(2,1)} %get-tuple-element.44.dqb_ref, ...), custom_call_target="tpu_custom_call" | custom-call | flops 25769803776 | bytes 67108864 | tf_op jit(solution)/shard_map/finish_grads/pallas_call | solution.py:700
  325.3 0.0 copy-done
  325.3 0.6 copy.15
  (1 shorter events, 0.0 us)
Async XLA Ops:
  284.4 40.9 %copy-start = (f32[1,2048]{1,0:T(1,128)S(1)}, f32[1,2048]{1,0:T(1,128)}, u32[]{:S(2)}) copy-start(f32[1,2048]{1,0:T(1,128)} %get-tuple-element.56) | copy-start | bytes 24580
